TPU v7x, 32 devices: a whole 2x2x4 slice. The times are simulated.
32 devices in a mesh: dp: 8 (over z, y), ctx: 4 (over x, core).
Axes of the slice: x: 2, y: 2, z: 4, core: 2. Of those that a mesh axis runs over, the one named last changes fastest.
Arguments:
- tokens: bfloat16 [16, 1024, 1024], P('dp', 'ctx'), may hold values from -6 to 6
- first_values: bfloat16 [16, 1024, 1024], P('dp', 'ctx'), may hold values from -6 to 6
- cotangent: bfloat16 [16, 1024, 1024], P('dp', 'ctx'), may hold values from -6 to 6
- segment_ids: int32 [16, 1024], P('dp'), may hold values from 0 to 4, as said below
- attn_gain: bfloat16 [1024], P(('dp', 'ctx')), may hold values from 0.5 to 1.5
- w_query: bfloat16 [1024, 1024], P(('dp', 'ctx')), may hold values from -0.1875 to 0.1875
- w_key: bfloat16 [1024, 1024], P(('dp', 'ctx')), may hold values from -0.1875 to 0.1875
- w_value: bfloat16 [1024, 1024], P(('dp', 'ctx')), may hold values from -0.1875 to 0.1875
- w_out: bfloat16 [1024, 1024], P(('dp', 'ctx')), may hold values from -1 to 1
- ffn_gain: bfloat16 [1024], P(('dp', 'ctx')), may hold values from 0.5 to 1.5
- gate_weight: bfloat16 [1024, 2816], P(('dp', 'ctx')), may hold values from -0.1875 to 0.1875
- up_weight: bfloat16 [1024, 2816], P(('dp', 'ctx')), may hold values from -0.1875 to 0.1875
- down_weight: bfloat16 [2816, 1024], P(('dp', 'ctx')), may hold values from -0.21875 to 0.21875
Outputs:
- output: bfloat16 [16, 1024, 1024], P('dp', 'ctx')
- tokens_grad: float32 [16, 1024, 1024], P('dp', 'ctx')
- first_values_grad: float32 [16, 1024, 1024], P('dp', 'ctx')
- attn_gain_grad: float32 [1024], P(('dp', 'ctx'))
- query_grad: float32 [1024, 1024], P(('dp', 'ctx'))
- key_grad: float32 [1024, 1024], P(('dp', 'ctx'))
- value_grad: float32 [1024, 1024], P(('dp', 'ctx'))
- out_grad: float32 [1024, 1024], P(('dp', 'ctx'))
- ffn_gain_grad: float32 [1024], P(('dp', 'ctx'))
- gate_grad: float32 [1024, 2816], P(('dp', 'ctx'))
- up_grad: float32 [1024, 2816], P(('dp', 'ctx'))
- down_grad: float32 [2816, 1024], P(('dp', 'ctx'))
Inputs may be any that keep to these rules, and one draw needn't show every extreme that they name: `segment_ids`: along each sequence the ids start at 0 and rise by one where a document begins; every document but a sequence's last holds 60 to 800 tokens, and each sequence holds at least one document of exactly 800 tokens.
All inputs are finite; a program needn't handle non-finite values.
Results may differ from a plain program's by a relative error of at most 0.017.
Values may be sent and summed in bfloat16 or wider, within the bound.
A program may use at most 192 MiB of HBM per device.

v0:
```python
import jax
import jax.numpy as jnp
from jax import lax
from jax.sharding import PartitionSpec as P

HEADS = 16
HEAD_DIM = 64
MICRO = 2


epsilon = 1e-05
rope_base = 10000.0
score_scale = 0.125
masked_score = -1e30


def inverse_rms(values):
    return lax.rsqrt(jnp.mean(values * values, axis=-1, keepdims=True) + epsilon)


def rotate(values, cos_table, sin_table):
    half_width = values.shape[-1] // 2
    first_half = values[..., :half_width]
    second_half = values[..., half_width:]
    return jnp.concatenate(
        [
            first_half * cos_table - second_half * sin_table,
            second_half * cos_table + first_half * sin_table,
        ],
        axis=-1,
    )


def unrotate(values, cos_table, sin_table):
    half_width = values.shape[-1] // 2
    first_half = values[..., :half_width]
    second_half = values[..., half_width:]
    return jnp.concatenate(
        [
            first_half * cos_table + second_half * sin_table,
            second_half * cos_table - first_half * sin_table,
        ],
        axis=-1,
    )


def swish(values):
    return values * jax.nn.sigmoid(values)


def layout(segments, ctx_rank, row_count):
    length = segments.shape[1]
    places = jnp.arange(length, dtype=jnp.int32)
    doc_edges = jnp.concatenate(
        [jnp.ones((segments.shape[0], 1), dtype=jnp.bool_), segments[:, 1:] != segments[:, :-1]],
        axis=1,
    )
    starts = lax.cummax(jnp.where(doc_edges, places[None, :], 0), axis=1)
    positions = places[None, :] - starts
    first_row = ctx_rank * row_count
    local_places = first_row + jnp.arange(row_count, dtype=jnp.int32)
    local_segments = lax.dynamic_slice_in_dim(segments, first_row, row_count, 1)
    local_positions = lax.dynamic_slice_in_dim(positions, first_row, row_count, 1)
    allowed = (local_segments[:, :, None] == segments[:, None, :]) & (
        places[None, None, :] <= local_places[None, :, None]
    )
    frequency = rope_base ** (-jnp.arange(HEAD_DIM // 2, dtype=jnp.float32) * 2.0 / HEAD_DIM)
    angles = local_positions.astype(jnp.float32)[:, :, None] * frequency
    return (allowed, jnp.cos(angles)[:, :, None, :], jnp.sin(angles)[:, :, None, :])


def weights_for(shards):
    attn_gain, w_query, w_key, w_value, w_out, ffn_gain, gate_weight, up_weight, down_weight = (
        shards
    )
    return (
        lax.all_gather(attn_gain, ("dp", "ctx"), axis=0, tiled=True),
        lax.all_gather(w_query, ("dp", "ctx"), axis=0, tiled=True),
        lax.all_gather(w_key, ("dp", "ctx"), axis=0, tiled=True),
        lax.all_gather(w_value, ("dp", "ctx"), axis=0, tiled=True),
        lax.all_gather(w_out, ("dp", "ctx"), axis=0, tiled=True),
        lax.all_gather(ffn_gain, ("dp", "ctx"), axis=0, tiled=True),
        lax.all_gather(gate_weight, ("dp", "ctx"), axis=0, tiled=True),
        lax.all_gather(up_weight, ("dp", "ctx"), axis=0, tiled=True),
        lax.all_gather(down_weight, ("dp", "ctx"), axis=0, tiled=True),
    )


def forward(full, tokens, first_values, allowed, cos_table, sin_table):
    attn_gain, w_query, w_key, w_value, w_out, ffn_gain, gate_weight, up_weight, down_weight = full
    seq_count, row_count, model_width = tokens.shape
    head_shape = (seq_count, row_count, HEADS, HEAD_DIM)
    tokens_float = tokens.astype(jnp.float32)
    scale_one = inverse_rms(tokens_float)
    normed_one = (tokens_float * scale_one * attn_gain.astype(jnp.float32)).astype(jnp.bfloat16)
    queries = jnp.einsum("mrd,de->mre", normed_one, w_query, preferred_element_type=jnp.float32)
    keys_lin = jnp.einsum("mrd,de->mre", normed_one, w_key, preferred_element_type=jnp.float32)
    values_lin = jnp.einsum("mrd,de->mre", normed_one, w_value, preferred_element_type=jnp.float32)
    query_rot = rotate(queries.reshape(head_shape), cos_table, sin_table).astype(jnp.bfloat16)
    key_rot = (
        rotate(keys_lin.reshape(head_shape), cos_table, sin_table)
        .astype(jnp.bfloat16)
        .reshape(seq_count, row_count, model_width)
    )
    values_mixed = (0.5 * values_lin + 0.5 * first_values.astype(jnp.float32)).astype(jnp.bfloat16)
    key_all, value_all = (
        lax.all_gather(key_rot, "ctx", axis=1, tiled=True),
        lax.all_gather(values_mixed, "ctx", axis=1, tiled=True),
    )
    length = key_all.shape[1]
    key_heads = key_all.reshape(seq_count, length, HEADS, HEAD_DIM)
    value_heads = value_all.reshape(seq_count, length, HEADS, HEAD_DIM)
    scores = (
        jnp.einsum("mqhd,mkhd->mhqk", query_rot, key_heads, preferred_element_type=jnp.float32)
        * score_scale
    )
    masked = jnp.where(allowed[:, None], scores, masked_score)
    row_peak = jnp.max(masked, axis=-1, keepdims=True)
    exp_terms = jnp.exp(masked - row_peak)
    row_total = jnp.sum(exp_terms, axis=-1, keepdims=True)
    attn_probs = exp_terms / row_total
    log_total = row_peak + jnp.log(row_total)
    attended = jnp.einsum(
        "mhqk,mkhd->mqhd",
        attn_probs.astype(jnp.bfloat16),
        value_heads,
        preferred_element_type=jnp.float32,
    )
    context = attended.astype(jnp.bfloat16).reshape(seq_count, row_count, model_width)
    residual = tokens_float + jnp.einsum(
        "mrd,de->mre", context, w_out, preferred_element_type=jnp.float32
    )
    scale_two = inverse_rms(residual)
    second_normed = (residual * scale_two * ffn_gain.astype(jnp.float32)).astype(jnp.bfloat16)
    gate_activation = jnp.einsum(
        "ajo,oc->ajc", second_normed, gate_weight, preferred_element_type=jnp.float32
    )
    up_activation = jnp.einsum(
        "ajo,oc->ajc", second_normed, up_weight, preferred_element_type=jnp.float32
    )
    hidden_product = (swish(gate_activation) * up_activation).astype(jnp.bfloat16)
    output = residual + jnp.einsum(
        "biu,ue->bie", hidden_product, down_weight, preferred_element_type=jnp.float32
    )
    kept = (
        tokens_float,
        scale_one,
        normed_one,
        query_rot,
        key_heads,
        value_heads,
        log_total,
        context,
        residual,
        scale_two,
        second_normed,
        gate_activation,
        up_activation,
        hidden_product,
    )
    return (output, kept)


def backward(full, kept, out_cotangent, allowed, cos_table, sin_table):
    attn_gain, w_query, w_key, w_value, w_out, ffn_gain, gate_weight, up_weight, down_weight = full
    (
        tokens_float,
        scale_one,
        normed_one,
        query_rot,
        key_heads,
        value_heads,
        log_total,
        context,
        residual,
        scale_two,
        second_normed,
        gate_activation,
        up_activation,
        hidden_product,
    ) = kept
    seq_count, row_count, model_width = residual.shape
    length = key_heads.shape[1]
    head_shape = (seq_count, row_count, HEADS, HEAD_DIM)
    out_float = out_cotangent.astype(jnp.float32)
    output_reduced = out_float.astype(jnp.bfloat16)
    down_weight_gradient = jnp.einsum(
        "tba,tby->ay", hidden_product, output_reduced, preferred_element_type=jnp.float32
    )
    hidden_cotangent = jnp.einsum(
        "voc,sc->vos", output_reduced, down_weight, preferred_element_type=jnp.float32
    )
    sigmoid_gate = jax.nn.sigmoid(gate_activation)
    gate_cotangent = (
        hidden_cotangent
        * up_activation
        * sigmoid_gate
        * (1.0 + gate_activation * (1.0 - sigmoid_gate))
    ).astype(jnp.bfloat16)
    up_cotangent = (hidden_cotangent * (gate_activation * sigmoid_gate)).astype(jnp.bfloat16)
    gate_weight_gradient = jnp.einsum(
        "noj,noa->ja", second_normed, gate_cotangent, preferred_element_type=jnp.float32
    )
    up_weight_gradient = jnp.einsum(
        "noj,noa->ja", second_normed, up_cotangent, preferred_element_type=jnp.float32
    )
    d_normed_two = jnp.einsum(
        "pvn,zn->pvz", gate_cotangent, gate_weight, preferred_element_type=jnp.float32
    ) + jnp.einsum("pvn,zn->pvz", up_cotangent, up_weight, preferred_element_type=jnp.float32)
    grad_ffn_gain = jnp.sum(d_normed_two * residual * scale_two, axis=(0, 1))
    weighted_two = d_normed_two * ffn_gain.astype(jnp.float32)
    d_residual = (
        out_float
        + scale_two * weighted_two
        - residual
        * (scale_two * scale_two * scale_two)
        * jnp.mean(weighted_two * residual, axis=-1, keepdims=True)
    )
    d_residual_low = d_residual.astype(jnp.bfloat16)
    grad_out = jnp.einsum(
        "mrd,mre->de", context, d_residual_low, preferred_element_type=jnp.float32
    )
    d_context = (
        jnp.einsum("mre,de->mrd", d_residual_low, w_out, preferred_element_type=jnp.float32)
        .astype(jnp.bfloat16)
        .reshape(head_shape)
    )
    scores = (
        jnp.einsum("mqhd,mkhd->mhqk", query_rot, key_heads, preferred_element_type=jnp.float32)
        * score_scale
    )
    masked = jnp.where(allowed[:, None], scores, masked_score)
    attn_probs = jnp.exp(masked - log_total)
    d_probs = jnp.einsum(
        "mqhd,mkhd->mhqk", d_context, value_heads, preferred_element_type=jnp.float32
    )
    value_part = jnp.einsum(
        "mhqk,mqhd->mkhd",
        attn_probs.astype(jnp.bfloat16),
        d_context,
        preferred_element_type=jnp.float32,
    )
    d_scores = (
        attn_probs * (d_probs - jnp.sum(d_probs * attn_probs, axis=-1, keepdims=True))
    ).astype(jnp.bfloat16)
    d_query_rot = (
        jnp.einsum("mhqk,mkhd->mqhd", d_scores, key_heads, preferred_element_type=jnp.float32)
        * score_scale
    )
    key_part = (
        jnp.einsum("mhqk,mqhd->mkhd", d_scores, query_rot, preferred_element_type=jnp.float32)
        * score_scale
    )
    d_key_rot, d_mixed = (
        lax.psum_scatter(
            key_part.reshape(seq_count, length, model_width).astype(jnp.bfloat16),
            "ctx",
            scatter_dimension=1,
            tiled=True,
        ).astype(jnp.float32),
        lax.psum_scatter(
            value_part.reshape(seq_count, length, model_width).astype(jnp.bfloat16),
            "ctx",
            scatter_dimension=1,
            tiled=True,
        ).astype(jnp.float32),
    )
    d_query = (
        unrotate(d_query_rot, cos_table, sin_table)
        .astype(jnp.bfloat16)
        .reshape(seq_count, row_count, model_width)
    )
    d_key = (
        unrotate(d_key_rot.reshape(head_shape), cos_table, sin_table)
        .astype(jnp.bfloat16)
        .reshape(seq_count, row_count, model_width)
    )
    d_value = (0.5 * d_mixed).astype(jnp.bfloat16)
    first_grad = 0.5 * d_mixed
    grad_query = jnp.einsum("mrd,mre->de", normed_one, d_query, preferred_element_type=jnp.float32)
    grad_key = jnp.einsum("mrd,mre->de", normed_one, d_key, preferred_element_type=jnp.float32)
    grad_value = jnp.einsum("mrd,mre->de", normed_one, d_value, preferred_element_type=jnp.float32)
    d_normed_one = jnp.einsum("mre,de->mrd", d_query, w_query, preferred_element_type=jnp.float32)
    d_normed_one = d_normed_one + jnp.einsum(
        "mre,de->mrd", d_key, w_key, preferred_element_type=jnp.float32
    )
    d_normed_one = d_normed_one + jnp.einsum(
        "mre,de->mrd", d_value, w_value, preferred_element_type=jnp.float32
    )
    grad_attn_gain = jnp.sum(d_normed_one * tokens_float * scale_one, axis=(0, 1))
    weighted_one = d_normed_one * attn_gain.astype(jnp.float32)
    token_grad = (
        d_residual
        + scale_one * weighted_one
        - tokens_float
        * (scale_one * scale_one * scale_one)
        * jnp.mean(weighted_one * tokens_float, axis=-1, keepdims=True)
    )
    grads = (
        grad_attn_gain,
        grad_query,
        grad_key,
        grad_value,
        grad_out,
        grad_ffn_gain,
        gate_weight_gradient,
        up_weight_gradient,
        down_weight_gradient,
    )
    return (token_grad, first_grad, grads)


def on_device(
    tokens,
    first_values,
    cotangent,
    segment_ids,
    attn_gain,
    w_query,
    w_key,
    w_value,
    w_out,
    ffn_gain,
    gate_weight,
    up_weight,
    down_weight,
):
    shards = (
        attn_gain,
        w_query,
        w_key,
        w_value,
        w_out,
        ffn_gain,
        gate_weight,
        up_weight,
        down_weight,
    )
    seq_count = tokens.shape[0] // MICRO
    row_count = tokens.shape[1]
    ctx_rank = lax.axis_index("ctx")
    outputs = []
    for micro_step in range(MICRO):
        begin_row = micro_step * seq_count
        end_row = begin_row + seq_count
        allowed, cos_table, sin_table = layout(segment_ids[begin_row:end_row], ctx_rank, row_count)
        full = weights_for(shards)
        output, kept = forward(
            full,
            tokens[begin_row:end_row],
            first_values[begin_row:end_row],
            allowed,
            cos_table,
            sin_table,
        )
        outputs.append(output.astype(jnp.bfloat16))
    token_grads = []
    first_grads = []
    summed = None
    for micro_step in range(MICRO):
        begin_row = micro_step * seq_count
        end_row = begin_row + seq_count
        allowed, cos_table, sin_table = layout(segment_ids[begin_row:end_row], ctx_rank, row_count)
        full = weights_for(shards)
        output, kept = forward(
            full,
            tokens[begin_row:end_row],
            first_values[begin_row:end_row],
            allowed,
            cos_table,
            sin_table,
        )
        token_grad, first_grad, grads = backward(
            full, kept, cotangent[begin_row:end_row], allowed, cos_table, sin_table
        )
        token_grads.append(token_grad)
        first_grads.append(first_grad)
        summed = grads if summed is None else jax.tree.map(jnp.add, summed, grads)
    (
        grad_attn_gain,
        grad_query,
        grad_key,
        grad_value,
        grad_out,
        grad_ffn_gain,
        gate_weight_gradient,
        up_weight_gradient,
        down_weight_gradient,
    ) = summed
    reduced = (
        lax.psum_scatter(grad_attn_gain, ("dp", "ctx"), scatter_dimension=0, tiled=True),
        lax.psum_scatter(grad_query, ("dp", "ctx"), scatter_dimension=0, tiled=True),
        lax.psum_scatter(grad_key, ("dp", "ctx"), scatter_dimension=0, tiled=True),
        lax.psum_scatter(grad_value, ("dp", "ctx"), scatter_dimension=0, tiled=True),
        lax.psum_scatter(grad_out, ("dp", "ctx"), scatter_dimension=0, tiled=True),
        lax.psum_scatter(grad_ffn_gain, ("dp", "ctx"), scatter_dimension=0, tiled=True),
        lax.psum_scatter(gate_weight_gradient, ("dp", "ctx"), scatter_dimension=0, tiled=True),
        lax.psum_scatter(up_weight_gradient, ("dp", "ctx"), scatter_dimension=0, tiled=True),
        lax.psum_scatter(down_weight_gradient, ("dp", "ctx"), scatter_dimension=0, tiled=True),
    )
    return (
        jnp.concatenate(outputs, axis=0),
        jnp.concatenate(token_grads, axis=0),
        jnp.concatenate(first_grads, axis=0),
        reduced[0],
        reduced[1],
        reduced[2],
        reduced[3],
        reduced[4],
        reduced[5],
        reduced[6],
        reduced[7],
        reduced[8],
    )


def solution(mesh):
    return jax.shard_map(
        on_device,
        mesh=mesh,
        in_specs=(
            P("dp", "ctx", None),
            P("dp", "ctx", None),
            P("dp", "ctx", None),
            P("dp", None),
            P(("dp", "ctx")),
            P(("dp", "ctx"), None),
            P(("dp", "ctx"), None),
            P(("dp", "ctx"), None),
            P(("dp", "ctx"), None),
            P(("dp", "ctx")),
            P(("dp", "ctx"), None),
            P(("dp", "ctx"), None),
            P(("dp", "ctx"), None),
        ),
        out_specs=(
            P("dp", "ctx", None),
            P("dp", "ctx", None),
            P("dp", "ctx", None),
            P(("dp", "ctx")),
            P(("dp", "ctx"), None),
            P(("dp", "ctx"), None),
            P(("dp", "ctx"), None),
            P(("dp", "ctx"), None),
            P(("dp", "ctx")),
            P(("dp", "ctx"), None),
            P(("dp", "ctx"), None),
            P(("dp", "ctx"), None),
        ),
        check_vma=False,
    )
```

profile of v0, /device:TPU:0, one launch (start us, length us, event | category | flops | bytes accessed | tf_op | source)
XLA Modules:
  0.0 1777.5 jit_solution(992295663132291391)
XLA Ops:
  11.1 42.1 %all-reduce.5 = (bf16[1024]{0:T(1024)(128)(2,1)S(1)}, bf16[1024]{0:T(1024)(128)(2,1)}) all-reduce(bf16[1024]{0:T(1024)(128)(2,1)S(1)} %dynamic-update-slice, bf16[1024]{0:T(1024)(128)(2,1)S(1)} %dynamic-update-slice.1), channel_id=1, replica_groups=mesh['dp'=8,'ctx'=4] {'dp','ctx'}, use_global_device_ids=true, to_apply=%add | all-reduce | flops 2048 | bytes 8192
  55.4 14.6 all-gather.12.cloned.1.call-done
  78.3 49.5 %all-gather.18.cloned.1.call-done = bf16[1024,1024]{1,0:T(8,128)(2,1)} async-done(((bf16[32,1024]{1,0:T(8,128)(2,1)}), bf16[1024,1024]{1,0:T(8,128)(2,1)}) %all-gather.18.cloned.1.call-update) | async-done | bytes 2097168 | tf_op jit(solution)/shard_map/all_gather | solution.py:79
  130.7 55.1 %all-gather.16.cloned.1.call-done = bf16[1024,1024]{1,0:T(8,128)(2,1)} async-done(((bf16[32,1024]{1,0:T(8,128)(2,1)}), bf16[1024,1024]{1,0:T(8,128)(2,1)}) %all-gather.16.cloned.1.call-update) | async-done | bytes 2097168 | tf_op jit(solution)/shard_map/all_gather | solution.py:78
  212.1 21.1 %all-gather.14.cloned.1.call-done = bf16[1,1024,1024]{2,1,0:T(8,128)(2,1)} async-done(((bf16[1,256,1024]{2,1,0:T(8,128)(2,1)}), bf16[1,1024,1024]{2,1,0:T(8,128)(2,1)}) %all-gather.14.cloned.1.call-update) | async-done | bytes 2097168 | tf_op jit(solution)/shard_map/all_gather | solution.py:108
  237.2 20.3 %all-gather.32.cloned.1.call-done = bf16[1,1024,1024]{1,2,0:T(8,128)(2,1)} async-done(((bf16[1,256,1024]{1,2,0:T(8,128)(2,1)}), bf16[1,1024,1024]{1,2,0:T(8,128)(2,1)}) %all-gather.32.cloned.1.call-update) | async-done | bytes 2097168 | tf_op jit(solution)/shard_map/all_gather | solution.py:107
  273.3 43.5 %all-gather.22.cloned.1.call-done = bf16[1024,1024]{1,0:T(8,128)(2,1)} async-done(((bf16[32,1024]{1,0:T(8,128)(2,1)}), bf16[1024,1024]{1,0:T(8,128)(2,1)}) %all-gather.22.cloned.1.call-update) | async-done | bytes 2097168 | tf_op jit(solution)/shard_map/all_gather | solution.py:81
  320.2 19.8 %all-gather.20.cloned.1.call-done = bf16[1,1024,1024]{1,2,0:T(8,128)(2,1)} async-done(((bf16[1,256,1024]{1,2,0:T(8,128)(2,1)}), bf16[1,1024,1024]{1,2,0:T(8,128)(2,1)}) %all-gather.20.cloned.1.call-update) | async-done | bytes 2097168 | tf_op jit(solution)/shard_map/all_gather | solution.py:107
  359.2 50.9 %all-gather.26.cloned.1.call-done = bf16[1024,2816]{1,0:T(8,128)(2,1)} async-done(((bf16[32,2816]{1,0:T(8,128)(2,1)}), bf16[1024,2816]{1,0:T(8,128)(2,1)}) %all-gather.26.cloned.1.call-update) | async-done | bytes 5767184 | tf_op jit(solution)/shard_map/all_gather | solution.py:84
  416.2 62.7 %all-gather.24.cloned.1.call-done = bf16[1024,2816]{1,0:T(8,128)(2,1)} async-done(((bf16[32,2816]{1,0:T(8,128)(2,1)}), bf16[1024,2816]{1,0:T(8,128)(2,1)}) %all-gather.24.cloned.1.call-update) | async-done | bytes 5767184 | tf_op jit(solution)/shard_map/all_gather | solution.py:83
  484.9 62.8 %all-gather.28.cloned.1.call-done = bf16[2816,1024]{1,0:T(8,128)(2,1)} async-done(((bf16[88,1024]{1,0:T(8,128)(2,1)}), bf16[2816,1024]{1,0:T(8,128)(2,1)}) %all-gather.28.cloned.1.call-update) | async-done | bytes 5767184 | tf_op jit(solution)/shard_map/all_gather | solution.py:85
  588.1 10.0 fusion.14
  607.0 9.4 fusion.17
  619.1 10.0 multiply_reduce_fusion
  640.9 10.3 multiply_reduce_fusion.1
  701.2 33.0 %reduce-scatter.12.cloned.1.call-done = bf16[1,256,1024]{1,2,0:T(8,128)(2,1)} async-done(((bf16[1,1024,1024]{1,2,0:T(8,128)(2,1)}), bf16[1,256,1024]{1,2,0:T(8,128)(2,1)}) %reduce-scatter.12.cloned.1.call-update) | async-done | bytes 524304 | tf_op jit(solution)/shard_map/reduce_scatter | solution.py:255
  797.8 39.7 %all-reduce.4 = (f32[1024]{0:T(1024)S(1)}, f32[1024]{0:T(1024)S(1)}) all-reduce(f32[1024]{0:T(1024)S(1)} %add.309, f32[1024]{0:T(1024)S(1)} %add.316), channel_id=6, replica_groups=mesh['dp'=8,'ctx'=4] {'dp','ctx'}, use_global_device_ids=true, to_apply=%region_24.25.clone | all-reduce | flops 2048 | bytes 16384
  843.9 36.0 %reduce-scatter.26.cloned.1.call-done = f32[32,1024]{1,0:T(8,128)} async-done(((f32[1024,1024]{1,0:T(8,128)}), f32[32,1024]{1,0:T(8,128)}) %reduce-scatter.26.cloned.1.call-update) | async-done | bytes 131088 | tf_op jit(solution)/shard_map/reduce_scatter | solution.py:395
  879.9 141.5 %reduce-scatter.24.cloned.1.call-done = f32[32,1024]{1,0:T(8,128)} async-done(((f32[1024,1024]{1,0:T(8,128)}), f32[32,1024]{1,0:T(8,128)}) %reduce-scatter.24.cloned.1.call-update) | async-done | bytes 131088 | tf_op jit(solution)/shard_map/reduce_scatter | solution.py:394
  1021.4 141.5 %reduce-scatter.22.cloned.1.call-done = f32[32,1024]{1,0:T(8,128)} async-done(((f32[1024,1024]{1,0:T(8,128)}), f32[32,1024]{1,0:T(8,128)}) %reduce-scatter.22.cloned.1.call-update) | async-done | bytes 131088 | tf_op jit(solution)/shard_map/reduce_scatter | solution.py:393
  1162.9 141.7 %reduce-scatter.20.cloned.1.call-done = f32[32,1024]{1,0:T(8,128)} async-done(((f32[1024,1024]{1,0:T(8,128)}), f32[32,1024]{1,0:T(8,128)}) %reduce-scatter.20.cloned.1.call-update) | async-done | bytes 131088 | tf_op jit(solution)/shard_map/reduce_scatter | solution.py:392
  1304.6 155.1 %reduce-scatter.30.cloned.1.call-done = f32[32,2816]{1,0:T(8,128)} async-done(((f32[1024,2816]{1,0:T(8,128)}), f32[32,2816]{1,0:T(8,128)}) %reduce-scatter.30.cloned.1.call-update) | async-done | bytes 360464 | tf_op jit(solution)/shard_map/reduce_scatter | solution.py:398
  1459.7 155.2 %reduce-scatter.28.cloned.1.call-done = f32[32,2816]{1,0:T(8,128)} async-done(((f32[1024,2816]{1,0:T(8,128)}), f32[32,2816]{1,0:T(8,128)}) %reduce-scatter.28.cloned.1.call-update) | async-done | bytes 360464 | tf_op jit(solution)/shard_map/reduce_scatter | solution.py:397
  1614.9 155.4 %reduce-scatter.32.cloned.1.call-done = f32[88,1024]{1,0:T(8,128)} async-done(((f32[2816,1024]{1,0:T(8,128)}), f32[88,1024]{1,0:T(8,128)}) %reduce-scatter.32.cloned.1.call-update) | async-done | bytes 360464 | tf_op jit(solution)/shard_map/reduce_scatter | solution.py:399
  (358 shorter events, 280.4 us)
Async XLA Ops:
  7.2 62.7 %all-gather.12.cloned.1.call-start = ((), (), s32[]{:S(2)}) async-start(), calls=%async_computation.11 | async-start | bytes 2162688 | tf_op jit(solution)/shard_map/all_gather | solution.py:80
  7.9 120.0 %all-gather.18.cloned.1.call-start = ((), (), s32[]{:S(2)}) async-start(), calls=%async_computation.14 | async-start | bytes 2162688 | tf_op jit(solution)/shard_map/all_gather | solution.py:79
  8.7 177.2 %all-gather.16.cloned.1.call-start = ((), (), s32[]{:S(2)}) async-start(), calls=%async_computation.13 | async-start | bytes 2162688 | tf_op jit(solution)/shard_map/all_gather | solution.py:78
  9.4 199.9 %all-gather.30.cloned.1.call-start = ((), (), s32[]{:S(2)}) async-start(), calls=%async_computation.20 | async-start | bytes 2621440 | tf_op jit(solution)/shard_map/all_gather | solution.py:108
  53.2 142.6 %copy-start.70 = (f32[1024]{0:T(1024)}, f32[1024]{0:T(1024)S(1)}, u32[]{:S(2)}) copy-start(f32[1024]{0:T(1024)S(1)} %convert_element_type.395) | copy-start | bytes 12292
  73.5 159.8 %all-gather.14.cloned.1.call-start = ((), (), s32[]{:S(2)}) async-start(), calls=%async_computation.12 | async-start | bytes 2621440 | tf_op jit(solution)/shard_map/all_gather | solution.py:108
  76.2 181.3 %all-gather.32.cloned.1.call-start = ((), (), s32[]{:S(2)}) async-start(), calls=%async_computation.21 | async-start | bytes 2621440 | tf_op jit(solution)/shard_map/all_gather | solution.py:107
  194.2 122.6 %all-gather.22.cloned.1.call-start = ((), (), s32[]{:S(2)}) async-start(), calls=%async_computation.16 | async-start | bytes 2162688 | tf_op jit(solution)/shard_map/all_gather | solution.py:81
  194.9 145.1 %all-gather.20.cloned.1.call-start = ((), (), s32[]{:S(2)}) async-start(), calls=%async_computation.15 | async-start | bytes 2621440 | tf_op jit(solution)/shard_map/all_gather | solution.py:107
  199.4 210.7 %all-gather.26.cloned.1.call-start = ((), (), s32[]{:S(2)}) async-start(), calls=%async_computation.18 | async-start | bytes 5947392 | tf_op jit(solution)/shard_map/all_gather | solution.py:84
  200.2 278.7 %all-gather.24.cloned.1.call-start = ((), (), s32[]{:S(2)}) async-start(), calls=%async_computation.17 | async-start | bytes 5947392 | tf_op jit(solution)/shard_map/all_gather | solution.py:83
  200.7 347.0 %all-gather.28.cloned.1.call-start = ((), (), s32[]{:S(2)}) async-start(), calls=%async_computation.19 | async-start | bytes 5947392 | tf_op jit(solution)/shard_map/all_gather | solution.py:85
  201.5 466.2 %reduce-scatter.14.cloned.1.call-start = ((), (), s32[]{:S(2)}) async-start(), calls=%async_computation.23 | async-start | bytes 2621440 | tf_op jit(solution)/shard_map/reduce_scatter | solution.py:261
  357.3 230.8 %copy-start.72 = (f32[16,256]{1,0:T(8,128)}, f32[16,256]{1,0:T(8,128)S(1)}, u32[]{:S(2)}) copy-start(f32[16,256]{1,0:T(8,128)S(1)} %log_add_fusion.1) | copy-start | bytes 49156
  602.1 70.0 %reduce-scatter.18.cloned.1.call-start = ((), (), s32[]{:S(2)}) async-start(), calls=%async_computation.25 | async-start | bytes 2621440 | tf_op jit(solution)/shard_map/reduce_scatter | solution.py:261
  619.0 81.1 %reduce-scatter.16.cloned.1.call-start = ((), (), s32[]{:S(2)}) async-start(), calls=%async_computation.24 | async-start | bytes 2621440 | tf_op jit(solution)/shard_map/reduce_scatter | solution.py:255
  640.9 93.3 %reduce-scatter.12.cloned.1.call-start = ((), (), s32[]{:S(2)}) async-start(), calls=%async_computation.22 | async-start | bytes 2621440 | tf_op jit(solution)/shard_map/reduce_scatter | solution.py:255
  662.9 217.0 %reduce-scatter.26.cloned.1.call-start = ((), (), s32[]{:S(2)}) async-start(), calls=%async_computation.29 | async-start | bytes 4325376 | tf_op jit(solution)/shard_map/reduce_scatter | solution.py:395
  667.6 353.8 %reduce-scatter.24.cloned.1.call-start = ((), (), s32[]{:S(2)}) async-start(), calls=%async_computation.28 | async-start | bytes 4325376 | tf_op jit(solution)/shard_map/reduce_scatter | solution.py:394
  677.8 485.2 %reduce-scatter.22.cloned.1.call-start = ((), (), s32[]{:S(2)}) async-start(), calls=%async_computation.27 | async-start | bytes 4325376 | tf_op jit(solution)/shard_map/reduce_scatter | solution.py:393
  742.7 561.9 %reduce-scatter.20.cloned.1.call-start = ((), (), s32[]{:S(2)}) async-start(), calls=%async_computation.26 | async-start | bytes 4325376 | tf_op jit(solution)/shard_map/reduce_scatter | solution.py:392
  748.8 710.9 %reduce-scatter.30.cloned.1.call-start = ((), (), s32[]{:S(2)}) async-start(), calls=%async_computation.31 | async-start | bytes 11894784 | tf_op jit(solution)/shard_map/reduce_scatter | solution.py:398
  758.9 856.0 %reduce-scatter.28.cloned.1.call-start = ((), (), s32[]{:S(2)}) async-start(), calls=%async_computation.30 | async-start | bytes 11894784 | tf_op jit(solution)/shard_map/reduce_scatter | solution.py:397
  768.2 1002.1 %reduce-scatter.32.cloned.1.call-start = ((), (), s32[]{:S(2)}) async-start(), calls=%async_computation.32 | async-start | bytes 11894784 | tf_op jit(solution)/shard_map/reduce_scatter | solution.py:399
  (89 other events, 1434.8 us)
Sparse Core Ops, SparseCore 0:
  10.8 59.0 all-gather.11
  72.8 55.0 all-gather.17
  130.7 55.0 all-gather.15
  187.8 21.4 all-gather.29
  210.7 22.5 all-gather.13
  234.7 22.8 all-gather.31
  260.4 56.3 all-gather.21
  318.3 21.6 all-gather.19
  342.8 67.2 all-gather.25
  412.8 65.9 all-gather.23
  481.7 65.9 all-gather.27
  602.2 29.8 reduce-scatter.13
  634.6 31.1 reduce-scatter.17
  668.8 31.2 reduce-scatter.15
  703.0 31.1 reduce-scatter.11
  736.9 142.9 reduce-scatter.25
  882.6 138.7 reduce-scatter.23
  1024.1 138.7 reduce-scatter.21
  1165.8 138.8 reduce-scatter.19
  1307.4 152.2 reduce-scatter.29
  1462.6 152.2 reduce-scatter.27
  1617.8 152.4 reduce-scatter.31
where the time goes:
time: 1790 us; the launch traced here: 1780 us
  waiting for transfers between devices  1380 us (77%)
  matrix products  208 us (12%)
  blocking collectives  81.8 us (5%)
  other arithmetic  48.9 us (3%)
  local copies, waits for them, and re-layouts  43.4 us (2%)
    reduce_scatter x1, waiting for transfers between devices, on_device(): lax.psum_scatter(down_weight_gradient, ('dp', 'ctx'), scatter_dimension=0...  155 us
    reduce_scatter x1, waiting for transfers between devices, on_device(): lax.psum_scatter(gate_weight_gradient, ('dp', 'ctx'), scatter_dimension=0...  155 us
    reduce_scatter x1, waiting for transfers between devices, on_device(): lax.psum_scatter(up_weight_gradient, ('dp', 'ctx'), scatter_dimension=0,...  155 us
    reduce_scatter x1, waiting for transfers between devices, on_device(): lax.psum_scatter(grad_query, ('dp', 'ctx'), scatter_dimension=0, tiled=True)  142 us
    reduce_scatter x1, waiting for transfers between devices, on_device(): lax.psum_scatter(grad_key, ('dp', 'ctx'), scatter_dimension=0, tiled=True)  142 us
    reduce_scatter x1, waiting for transfers between devices, on_device(): lax.psum_scatter(grad_value, ('dp', 'ctx'), scatter_dimension=0, tiled=True)  142 us
    unnamed x2, blocking collectives  81.8 us
    all_gather x1, waiting for transfers between devices, weights_for(): lax.all_gather(down_weight, ('dp', 'ctx'), axis=0, tiled=True)  62.8 us
  transfers between devices with their start and end apart: 22, of which 20 were waited for; matrix products, arithmetic and copies ran while one was open for 13% of the time, Pallas kernels for 0%

commit v1 on v0

v1 whole, which is shorter than its diff:
```python
import functools
import jax
import jax.numpy as jnp
from jax import lax
from jax.experimental import pallas as pl
from jax.experimental.pallas import tpu as pltpu
from jax.sharding import PartitionSpec as P

HEADS = 16
HEAD_DIM = 64
MESH_ID = pl.DeviceIdType.MESH

epsilon = 1e-05
rope_base = 10000.0
score_scale = 0.125
masked_score = -1e30


def inverse_rms(values):
    return lax.rsqrt(jnp.mean(values * values, axis=-1, keepdims=True) + epsilon)


def rotate(values, cos_table, sin_table):
    half_width = values.shape[-1] // 2
    first_half = values[..., :half_width]
    second_half = values[..., half_width:]
    return jnp.concatenate(
        [
            first_half * cos_table - second_half * sin_table,
            second_half * cos_table + first_half * sin_table,
        ],
        axis=-1,
    )


def unrotate(values, cos_table, sin_table):
    half_width = values.shape[-1] // 2
    first_half = values[..., :half_width]
    second_half = values[..., half_width:]
    return jnp.concatenate(
        [
            first_half * cos_table + second_half * sin_table,
            second_half * cos_table - first_half * sin_table,
        ],
        axis=-1,
    )


def swish(values):
    return values * jax.nn.sigmoid(values)


def layout(segments, ctx_rank, row_count):
    length = segments.shape[1]
    places = jnp.arange(length, dtype=jnp.int32)
    doc_edges = jnp.concatenate(
        [jnp.ones((segments.shape[0], 1), dtype=jnp.bool_), segments[:, 1:] != segments[:, :-1]],
        axis=1,
    )
    starts = lax.cummax(jnp.where(doc_edges, places[None, :], 0), axis=1)
    positions = places[None, :] - starts
    first_row = ctx_rank * row_count
    local_places = first_row + jnp.arange(row_count, dtype=jnp.int32)
    local_segments = lax.dynamic_slice_in_dim(segments, first_row, row_count, 1)
    local_positions = lax.dynamic_slice_in_dim(positions, first_row, row_count, 1)
    allowed = (local_segments[:, :, None] == segments[:, None, :]) & (
        places[None, None, :] <= local_places[None, :, None]
    )
    frequency = rope_base ** (-jnp.arange(HEAD_DIM // 2, dtype=jnp.float32) * 2.0 / HEAD_DIM)
    angles = local_positions.astype(jnp.float32)[:, :, None] * frequency
    return (allowed, jnp.cos(angles)[:, :, None, :], jnp.sin(angles)[:, :, None, :])


def position():
    dp = lax.axis_index("dp")
    ct = lax.axis_index("ctx")
    return lax.div(dp, 2), lax.rem(dp, 2), lax.div(ct, 2), lax.rem(ct, 2)


def visit(step, z, planes):
    back = planes - 1 - step
    high = back + jnp.where(back >= z, 1, 0)
    low = planes - 1 - back
    low = low - jnp.where(low <= z, 1, 0)
    other = jnp.where(z < planes // 2, low, high)
    return jnp.where(step == 0, z, other)


def device(z, y, x, c):
    return (z * 2 + y, x * 2 + c)


def halves(shape):
    if shape[0] % 2 == 0:
        cut = shape[0] // 2
        return (pl.ds(0, cut), slice(None), slice(None)), (pl.ds(cut, cut), slice(None), slice(None))
    cut = shape[2] // 2 // 128 * 128
    return (
        (slice(None), slice(None), pl.ds(0, cut)),
        (slice(None), slice(None), pl.ds(cut, shape[2] - cut)),
    )


def entry_barrier(z, y, x, c, planes):
    barrier = pltpu.get_barrier_semaphore()

    def hello(target):
        pl.semaphore_signal(barrier, inc=1, device_id=target, device_id_type=MESH_ID)

    hello(device(z, y, 1 - x, c))
    hello(device(z, 1 - y, x, c))
    hello(device(z, y, x, 1 - c))

    @pl.when(z > 0)
    def _():
        hello(device(z - 1, y, x, c))

    @pl.when(z < planes - 1)
    def _():
        hello(device(z + 1, y, x, c))

    pl.semaphore_wait(barrier, 3 + jnp.where(z > 0, 1, 0) + jnp.where(z < planes - 1, 1, 0))


def gather_kernel(planes, shapes, *refs):
    n = len(shapes)
    ins, outs, sems = refs[:n], refs[n : 2 * n], refs[2 * n :]
    own_sem, z_send, z_recv, x_send, x_recv, y_send, y_recv, d_send, d_recv, c_send, c_recv = sems
    z, y, x, c = position()
    entry_barrier(z, y, x, c, planes)
    local = [
        pltpu.make_async_copy(ins[g], outs[g].at[:, z, y, x, c], own_sem.at[g]) for g in range(n)
    ]
    for copy in local:
        copy.start()

    def push(src, dst, send, recv, target):
        return pltpu.make_async_remote_copy(
            src_ref=src,
            dst_ref=dst,
            send_sem=send,
            recv_sem=recv,
            device_id=target,
            device_id_type=MESH_ID,
        )

    def spot(g, zz, yy, xx):
        return outs[g].at[:, zz, yy, xx, c]

    def z_copy(g, zz, up, own):
        side = 1 if up else 0
        return push(
            ins[g] if own else spot(g, zz, y, x),
            spot(g, zz, y, x),
            z_send.at[g, zz, side],
            z_recv.at[g, zz],
            device(z + 1 if up else z - 1, y, x, c),
        )

    def x_copy(g, zz, own):
        return push(
            ins[g] if own else spot(g, zz, y, x),
            spot(g, zz, y, x),
            x_send.at[g, zz],
            x_recv.at[g, zz],
            device(z, y, 1 - x, c),
        )

    def y_copy(g, zz, own):
        return push(
            ins[g] if own else spot(g, zz, y, x),
            spot(g, zz, y, x),
            y_send.at[g, zz],
            y_recv.at[g, zz],
            device(z, 1 - y, x, c),
        )

    def relay(g, zz, half):
        part = halves(shapes[g])[half]
        if half == 0:
            here, target = spot(g, zz, y, 1 - x), device(z, 1 - y, x, c)
        else:
            here, target = spot(g, zz, 1 - y, x), device(z, y, 1 - x, c)
        here = here.at[part]
        return push(here, here, d_send.at[g, zz, half], d_recv.at[g, zz, half], target)

    def diag_arrival(g, zz, half):
        part = halves(shapes[g])[half]
        here = spot(g, zz, 1 - y, 1 - x).at[part]
        return push(
            here, here, d_send.at[g, zz, half], d_recv.at[g, zz, half], device(z, y, x, 1 - c)
        )

    def core_copy(g, zz, mine):
        here = outs[g].at[:, zz, :, :, c if mine else 1 - c]
        return push(here, here, c_send.at[g, zz], c_recv.at[g, zz], device(z, y, x, 1 - c))

    def spread(g, zz, own):
        if own:

            @pl.when(z > 0)
            def _():
                z_copy(g, zz, False, True).start()

            @pl.when(z < planes - 1)
            def _():
                z_copy(g, zz, True, True).start()

        else:

            @pl.when((zz < z) & (z < planes - 1))
            def _():
                z_copy(g, zz, True, False).start()

            @pl.when((zz > z) & (z > 0))
            def _():
                z_copy(g, zz, False, False).start()

        x_copy(g, zz, own).start()
        y_copy(g, zz, own).start()

    items = [(t, g) for t in range(planes) for g in range(n)]
    lag_plane, lag_core = n, 2 * n

    def stage_plane(t, g):
        zz = visit(t, z, planes)
        x_copy(g, zz, False).wait_recv()
        relay(g, zz, 0).start()
        y_copy(g, zz, False).wait_recv()
        relay(g, zz, 1).start()

    def stage_core(t, g):
        zz = visit(t, z, planes)
        if t == 0:
            local[g].wait()
        diag_arrival(g, zz, 0).wait_recv()
        diag_arrival(g, zz, 1).wait_recv()
        core_copy(g, zz, True).start()

    for i in range(len(items) + lag_core):
        if i < len(items):
            t, g = items[i]
            zz = visit(t, z, planes)
            if t > 0:
                z_copy(g, zz, True, False).wait_recv()
            spread(g, zz, t == 0)
        if 0 <= i - lag_plane < len(items):
            stage_plane(*items[i - lag_plane])
        if 0 <= i - lag_core < len(items):
            stage_core(*items[i - lag_core])
    for t, g in items:
        zz = visit(t, z, planes)
        core_copy(g, zz, False).wait_recv()
        core_copy(g, zz, True).wait_send()
        x_copy(g, zz, t == 0).wait_send()
        y_copy(g, zz, t == 0).wait_send()
        relay(g, zz, 0).wait_send()
        relay(g, zz, 1).wait_send()
        if t == 0:

            @pl.when(z > 0)
            def _():
                z_copy(g, zz, False, True).wait_send()

            @pl.when(z < planes - 1)
            def _():
                z_copy(g, zz, True, True).wait_send()

        else:

            @pl.when((zz < z) & (z < planes - 1))
            def _():
                z_copy(g, zz, True, False).wait_send()

            @pl.when((zz > z) & (z > 0))
            def _():
                z_copy(g, zz, False, False).wait_send()


def gather(planes, blocks):
    n = len(blocks)
    shapes = [b.shape for b in blocks]
    dma = pltpu.SemaphoreType.DMA
    return pl.pallas_call(
        functools.partial(gather_kernel, planes, shapes),
        out_shape=[
            jax.ShapeDtypeStruct((s[0], planes, 2, 2, 2, s[1], s[2]), b.dtype)
            for s, b in zip(shapes, blocks)
        ],
        in_specs=[pl.BlockSpec(memory_space=pl.ANY)] * n,
        out_specs=[pl.BlockSpec(memory_space=pl.ANY)] * n,
        scratch_shapes=[
            dma((n,)),
            dma((n, planes, 2)),
            dma((n, planes)),
            dma((n, planes)),
            dma((n, planes)),
            dma((n, planes)),
            dma((n, planes)),
            dma((n, planes, 2)),
            dma((n, planes, 2)),
            dma((n, planes)),
            dma((n, planes)),
        ],
        compiler_params=pltpu.CompilerParams(collective_id=0, has_side_effects=True),
        name="weight_gather",
    )(*blocks)


def columns(shape, half):
    cut = shape[1] // 2 // 128 * 128
    return pl.ds(0, cut) if half == 0 else pl.ds(cut, shape[1] - cut)


def scatter_kernel(planes, shapes, lags, *refs):
    n = len(shapes)
    parts, outs, refs = refs[:n], refs[n : 2 * n], refs[2 * n :]
    own, from_core, from_dx, from_dy, from_x, from_y, from_z = (
        refs[k * n : (k + 1) * n] for k in range(7)
    )
    own_sem, c_send, c_recv, d_send, d_recv, x_send, x_recv, y_send, y_recv, z_send, z_recv = refs[
        7 * n :
    ]
    z, y, x, c = position()
    entry_barrier(z, y, x, c, planes)
    items = [(planes - 1 - t, g) for t in range(planes) for g in range(n)]

    def push(src, dst, send, recv, target):
        return pltpu.make_async_remote_copy(
            src_ref=src,
            dst_ref=dst,
            send_sem=send,
            recv_sem=recv,
            device_id=target,
            device_id_type=MESH_ID,
        )

    def load(g, zz):
        return pltpu.make_async_copy(
            parts[g].at[zz, :, :, c], own[g].at[zz], own_sem.at[g, zz]
        )

    def core_copy(g, zz):
        return push(
            parts[g].at[zz, :, :, 1 - c],
            from_core[g].at[zz],
            c_send.at[g, zz],
            c_recv.at[g, zz],
            device(z, y, x, 1 - c),
        )

    def diag(g, zz, half):
        part = columns(shapes[g], half)
        box = (from_dx if half == 0 else from_dy)[g].at[zz]
        return push(
            own[g].at[zz, 1 - y, 1 - x, :, part],
            box,
            d_send.at[g, zz, half],
            d_recv.at[g, zz, half],
            device(z, y, 1 - x, c) if half == 0 else device(z, 1 - y, x, c),
        )

    def x_copy(g, zz):
        return push(
            own[g].at[zz, y, 1 - x],
            from_x[g].at[zz],
            x_send.at[g, zz],
            x_recv.at[g, zz],
            device(z, y, 1 - x, c),
        )

    def y_copy(g, zz):
        return push(
            own[g].at[zz, 1 - y, x],
            from_y[g].at[zz],
            y_send.at[g, zz],
            y_recv.at[g, zz],
            device(z, 1 - y, x, c),
        )

    def z_copy(g, zz, up):
        slot = zz if up else jnp.where(zz == z - 1, planes, zz)
        return push(
            own[g].at[zz, y, x],
            from_z[g].at[slot],
            z_send.at[g, zz],
            z_recv.at[g, slot],
            device(z + 1 if up else z - 1, y, x, c),
        )

    def z_arrival(g, slot):
        return push(
            from_z[g].at[slot],
            from_z[g].at[slot],
            z_send.at[g, 0],
            z_recv.at[g, slot],
            device(z, y, x, 1 - c),
        )

    f32 = jnp.float32

    def add(dst, *srcs):
        total = dst[...].astype(f32)
        for src in srcs:
            total = total + src[...].astype(f32)
        dst[...] = total.astype(dst.dtype)

    for t, g in items:
        zz = visit(t, z, planes)
        core_copy(g, zz).start()
        load(g, zz).start()

    def stage_core(t, g):
        zz = visit(t, z, planes)
        load(g, zz).wait()
        core_copy(g, zz).wait_recv()
        add(own[g].at[zz, 1 - y, 1 - x], from_core[g].at[zz, 1 - y, 1 - x])
        diag(g, zz, 0).start()
        diag(g, zz, 1).start()
        add(own[g].at[zz, y, 1 - x], from_core[g].at[zz, y, 1 - x])
        add(own[g].at[zz, 1 - y, x], from_core[g].at[zz, 1 - y, x])
        add(own[g].at[zz, y, x], from_core[g].at[zz, y, x])

    def stage_plane(t, g):
        zz = visit(t, z, planes)
        diag(g, zz, 0).wait_recv()
        add(own[g].at[zz, 1 - y, x, :, columns(shapes[g], 0)], from_dx[g].at[zz])
        y_copy(g, zz).start()
        diag(g, zz, 1).wait_recv()
        add(own[g].at[zz, y, 1 - x, :, columns(shapes[g], 1)], from_dy[g].at[zz])
        x_copy(g, zz).start()

    def stage_line(t, g):
        zz = visit(t, z, planes)
        x_copy(g, zz).wait_recv()
        y_copy(g, zz).wait_recv()
        here = own[g].at[zz, y, x]
        if t > 0:
            add(here, from_x[g].at[zz], from_y[g].at[zz])
            farther = jnp.where(zz > z, z > 0, z < planes - 1)

            @pl.when(farther)
            def _():
                z_arrival(g, zz).wait_recv()
                add(here, from_z[g].at[zz])

            @pl.when(zz > z)
            def _():
                z_copy(g, zz, True).start()

            @pl.when(zz < z)
            def _():
                z_copy(g, zz, False).start()

        else:
            outs[g][...] = (
                here[...].astype(f32)
                + from_x[g][zz].astype(f32)
                + from_y[g][zz].astype(f32)
            )

            @pl.when(z > 0)
            def _():
                z_arrival(g, zz).wait_recv()
                outs[g][...] += from_z[g][zz].astype(f32)

            @pl.when(z < planes - 1)
            def _():
                z_arrival(g, planes).wait_recv()
                outs[g][...] += from_z[g][planes].astype(f32)

    lag_plane, lag_line = lags
    for i in range(len(items) + lag_line):
        if i < len(items):
            stage_core(*items[i])
        if 0 <= i - lag_plane < len(items):
            stage_plane(*items[i - lag_plane])
        if 0 <= i - lag_line < len(items):
            stage_line(*items[i - lag_line])
    for t, g in items:
        zz = visit(t, z, planes)
        core_copy(g, zz).wait_send()
        diag(g, zz, 0).wait_send()
        diag(g, zz, 1).wait_send()
        x_copy(g, zz).wait_send()
        y_copy(g, zz).wait_send()
        if t > 0:
            z_copy(g, zz, True).wait_send()


def scatter_sum(planes, partials, lags, collective_id=1):
    n = len(partials)
    shapes = [p.shape[4:] for p in partials]
    types = [p.dtype for p in partials]
    dma = pltpu.SemaphoreType.DMA

    def boxes(lead, half=None):
        out = []
        for s, d in zip(shapes, types):
            cut = s[1] // 2 // 128 * 128
            width = s[1] if half is None else (cut if half == 0 else s[1] - cut)
            out.append(pltpu.VMEM((*lead, s[0], width), d))
        return out

    return pl.pallas_call(
        functools.partial(scatter_kernel, planes, shapes, lags),
        out_shape=[jax.ShapeDtypeStruct(s, jnp.float32) for s in shapes],
        in_specs=[pl.BlockSpec(memory_space=pl.ANY)] * n,
        out_specs=[pl.BlockSpec(memory_space=pltpu.VMEM)] * n,
        scratch_shapes=[
            *boxes((planes, 2, 2)),
            *boxes((planes, 2, 2)),
            *boxes((planes,), 0),
            *boxes((planes,), 1),
            *boxes((planes,)),
            *boxes((planes,)),
            *boxes((planes + 1,)),
            dma((n, planes)),
            dma((n, planes)),
            dma((n, planes)),
            dma((n, planes, 2)),
            dma((n, planes, 2)),
            dma((n, planes)),
            dma((n, planes)),
            dma((n, planes)),
            dma((n, planes)),
            dma((n, planes)),
            dma((n, planes + 1)),
        ],
        compiler_params=pltpu.CompilerParams(
            collective_id=collective_id, has_side_effects=True, vmem_limit_bytes=62 * 2**20
        ),
        name="gradient_scatter",
    )(*partials)


X_SEND = ((0, 2), (1, 3))
X_BACK = ((2, 0), (3, 1))
CORES = ((0, 1), (1, 0), (2, 3), (3, 2))


def share_keys(pair):
    rank = lax.axis_index("ctx")
    from_x = lax.ppermute(pair, "ctx", X_SEND)
    both = jnp.stack([pair, from_x])
    other = lax.ppermute(both, "ctx", CORES)
    odd = rank % 2 == 1
    high = rank >= 2
    first = jnp.where(odd, other, both)
    second = jnp.where(odd, both, other)
    zero = jnp.zeros_like(first[0])
    tiles = [
        jnp.where(high, first[1], first[0]),
        jnp.where(high, second[1], second[0]),
        jnp.where(high, first[0], zero),
        jnp.where(high, second[0], zero),
    ]
    return jnp.concatenate(tiles, axis=2)


def return_sums(pair):
    rank = lax.axis_index("ctx")
    rows = pair.shape[2] // 4
    odd = rank % 2 == 1
    high = rank >= 2
    tiles = [pair[:, :, i * rows : (i + 1) * rows] for i in range(4)]
    low = pair.dtype
    mine = jnp.stack(
        [jnp.where(odd, tiles[1], tiles[0]), jnp.where(odd, tiles[3], tiles[2])]
    )
    theirs = jnp.stack(
        [jnp.where(odd, tiles[0], tiles[1]), jnp.where(odd, tiles[2], tiles[3])]
    )
    got = lax.ppermute(theirs, "ctx", CORES)
    chip = mine.astype(jnp.float32) + got.astype(jnp.float32)
    back = lax.ppermute(chip[0].astype(low), "ctx", X_BACK)
    return jnp.where(high, chip[1], chip[0]) + back.astype(jnp.float32)


def on_device(
    planes,
    tokens,
    first_values,
    cotangent,
    segment_ids,
    attn_gain,
    w_query,
    w_key,
    w_value,
    w_out,
    ffn_gain,
    gate_weight,
    up_weight,
    down_weight,
):
    f32, bf16 = jnp.float32, jnp.bfloat16
    devices = planes * 8
    seqs, rows, width = tokens.shape
    rank = lax.axis_index("ctx")
    share = attn_gain.shape[0]
    gains = jnp.zeros((1, 16, 128), bf16)
    gains = gains.at[0, 0, :share].set(attn_gain).at[0, 1, :share].set(ffn_gain)
    shards = (gains, w_query, w_key, w_value, w_out, gate_weight, up_weight, down_weight)
    blocks = [s if s.ndim == 3 else s[None] for s in shards]
    gathered = gather(planes, blocks)
    gain_all = gathered[0].reshape(devices, 16, 128)
    attn_gain = gain_all[:, 0, :share].reshape(width)
    ffn_gain = gain_all[:, 1, :share].reshape(width)
    w_query, w_key, w_value, w_out, gate_weight, up_weight, down_weight = (
        g.reshape(devices * b.shape[1], b.shape[2]) for g, b in zip(gathered[1:], blocks[1:])
    )
    allowed, cos_table, sin_table = layout(segment_ids, rank, rows)

    head_shape = (seqs, rows, HEADS, HEAD_DIM)
    mm = functools.partial(jnp.einsum, preferred_element_type=f32)
    tokens_float = tokens.astype(f32)
    scale_one = inverse_rms(tokens_float)
    normed_one = (tokens_float * scale_one * attn_gain.astype(f32)).astype(bf16)
    queries = mm("mrd,de->mre", normed_one, w_query)
    keys_lin = mm("mrd,de->mre", normed_one, w_key)
    values_lin = mm("mrd,de->mre", normed_one, w_value)
    query_rot = rotate(queries.reshape(head_shape), cos_table, sin_table).astype(bf16)
    key_rot = rotate(keys_lin.reshape(head_shape), cos_table, sin_table).astype(bf16)
    values_mixed = (0.5 * values_lin + 0.5 * first_values.astype(f32)).astype(bf16)
    pair = share_keys(jnp.stack([key_rot.reshape(seqs, rows, width), values_mixed]))
    length = pair.shape[2]
    key_heads = pair[0].reshape(seqs, length, HEADS, HEAD_DIM)
    value_heads = pair[1].reshape(seqs, length, HEADS, HEAD_DIM)
    scores = mm("mqhd,mkhd->mhqk", query_rot, key_heads) * score_scale
    masked = jnp.where(allowed[:, None], scores, masked_score)
    row_peak = jnp.max(masked, axis=-1, keepdims=True)
    exp_terms = jnp.exp(masked - row_peak)
    row_total = jnp.sum(exp_terms, axis=-1, keepdims=True)
    attn_probs = exp_terms / row_total
    attended = mm("mhqk,mkhd->mqhd", attn_probs.astype(bf16), value_heads)
    context = attended.astype(bf16).reshape(seqs, rows, width)
    residual = tokens_float + mm("mrd,de->mre", context, w_out)
    scale_two = inverse_rms(residual)
    second_normed = (residual * scale_two * ffn_gain.astype(f32)).astype(bf16)
    gate = mm("ajo,oc->ajc", second_normed, gate_weight)
    up = mm("ajo,oc->ajc", second_normed, up_weight)
    hidden = (swish(gate) * up).astype(bf16)
    output = (residual + mm("biu,ue->bie", hidden, down_weight)).astype(bf16)

    out_float = cotangent.astype(f32)
    d_down = mm("tba,tby->ay", hidden, cotangent).astype(bf16)
    d_hidden = mm("voc,sc->vos", cotangent, down_weight)
    sigmoid_gate = jax.nn.sigmoid(gate)
    d_gate = (d_hidden * up * sigmoid_gate * (1.0 + gate * (1.0 - sigmoid_gate))).astype(bf16)
    d_up = (d_hidden * (gate * sigmoid_gate)).astype(bf16)
    d_gate_weight = mm("noj,noa->ja", second_normed, d_gate).astype(bf16)
    d_up_weight = mm("noj,noa->ja", second_normed, d_up).astype(bf16)
    d_normed_two = mm("pvn,zn->pvz", d_gate, gate_weight) + mm("pvn,zn->pvz", d_up, up_weight)
    d_ffn_gain = jnp.sum(d_normed_two * residual * scale_two, axis=(0, 1))
    weighted_two = d_normed_two * ffn_gain.astype(f32)
    d_residual = (
        out_float
        + scale_two * weighted_two
        - residual
        * (scale_two * scale_two * scale_two)
        * jnp.mean(weighted_two * residual, axis=-1, keepdims=True)
    )
    d_residual_low = d_residual.astype(bf16)
    d_out = mm("mrd,mre->de", context, d_residual_low).astype(bf16)
    d_context = mm("mre,de->mrd", d_residual_low, w_out).astype(bf16).reshape(head_shape)
    d_probs = mm("mqhd,mkhd->mhqk", d_context, value_heads)
    value_part = mm("mhqk,mqhd->mkhd", attn_probs.astype(bf16), d_context)
    d_scores = (
        attn_probs * (d_probs - jnp.sum(d_probs * attn_probs, axis=-1, keepdims=True))
    ).astype(bf16)
    d_query_rot = mm("mhqk,mkhd->mqhd", d_scores, key_heads) * score_scale
    key_part = mm("mhqk,mqhd->mkhd", d_scores, query_rot) * score_scale
    flat = (seqs, length, width)
    d_pair = return_sums(jnp.stack([key_part.reshape(flat), value_part.reshape(flat)]).astype(bf16))
    d_key_rot, d_mixed = d_pair[0], d_pair[1]
    local = (seqs, rows, width)
    d_query = unrotate(d_query_rot, cos_table, sin_table).astype(bf16).reshape(local)
    d_key = (
        unrotate(d_key_rot.reshape(head_shape), cos_table, sin_table).astype(bf16).reshape(local)
    )
    d_value = (0.5 * d_mixed).astype(bf16)
    first_grad = 0.5 * d_mixed
    d_wq = mm("mrd,mre->de", normed_one, d_query).astype(bf16)
    d_wk = mm("mrd,mre->de", normed_one, d_key).astype(bf16)
    d_wv = mm("mrd,mre->de", normed_one, d_value).astype(bf16)
    d_normed_one = (
        mm("mre,de->mrd", d_query, w_query)
        + mm("mre,de->mrd", d_key, w_key)
        + mm("mre,de->mrd", d_value, w_value)
    )
    d_attn_gain = jnp.sum(d_normed_one * tokens_float * scale_one, axis=(0, 1))
    weighted_one = d_normed_one * attn_gain.astype(f32)
    token_grad = (
        d_residual
        + scale_one * weighted_one
        - tokens_float
        * (scale_one * scale_one * scale_one)
        * jnp.mean(weighted_one * tokens_float, axis=-1, keepdims=True)
    )
    d_gains = jnp.stack([d_attn_gain, d_ffn_gain]).reshape(2, devices, share)
    d_gains = jnp.zeros((devices, 8, 256), f32).at[:, :2, :share].set(d_gains.transpose(1, 0, 2))
    partials = [
        g.reshape(planes, 2, 2, 2, g.size // g.shape[-1] // devices, g.shape[-1])
        for g in (d_down, d_gate_weight, d_up_weight, d_out, d_wq, d_wk, d_wv, d_gains)
    ]
    s_down, s_gate, s_up, s_out, s_wq, s_wk, s_wv, s_gains = scatter_sum(planes, partials, (4, 8))
    return (
        output,
        token_grad,
        first_grad,
        s_gains[0, :share],
        s_wq,
        s_wk,
        s_wv,
        s_out,
        s_gains[1, :share],
        s_gate,
        s_up,
        s_down,
    )


def solution(mesh):
    token, weight, vector = P("dp", "ctx", None), P(("dp", "ctx"), None), P(("dp", "ctx"))
    return jax.shard_map(
        functools.partial(on_device, mesh.shape["dp"] // 2),
        mesh=mesh,
        in_specs=(
            token,
            token,
            token,
            P("dp", None),
            vector,
            weight,
            weight,
            weight,
            weight,
            vector,
            weight,
            weight,
            weight,
        ),
        out_specs=(
            token,
            token,
            token,
            vector,
            weight,
            weight,
            weight,
            weight,
            vector,
            weight,
            weight,
            weight,
        ),
        check_vma=False,
    )
```

time: 1790 us -> 631 us (0.35)
  waiting for transfers between devices: 1380 us -> 75.1 us
  Pallas kernels: 0 us -> 229 us
  blocking collectives: 81.8 us -> 0 us
  matrix products: 208 us -> 183 us
  other arithmetic: 48.9 us -> 70.7 us
    reduce_scatter x11 -> x0, waiting for transfers between devices: 967 us -> none  [the longest x1 155 us: on_device(): lax.psum_scatter(down_weight_gradient, ('dp', 'ctx'), scatter_dimension=0...]
    all_gather x11 -> x0, waiting for transfers between devices: 406 us -> none  [the longest x1 62.8 us: weights_for(): lax.all_gather(down_weight, ('dp', 'ctx'), axis=0, tiled=True)]
    pallas_call x0 -> x2, Pallas kernels: none -> 229 us  [the longest x1 115 us: gather(): pl.pallas_call(functools.partial(gather_kernel, planes, shapes), out_shap...]
    unnamed x2 -> x0, blocking collectives: 81.8 us -> none
    ppermute x0 -> x4, waiting for transfers between devices: none -> 75.1 us  [the longest x1 45.3 us: share_keys(): from_x = lax.ppermute(pair, 'ctx', X_SEND)]
    dot_general x54 -> x26, matrix products: 208 us -> 164 us  [the longest x1 23 us: on_device(): d_probs = mm('mqhd,mkhd->mhqk', d_context, value_heads)]
    sub x0 -> x1, matrix products: none -> 19.1 us  [on_device(): exp_terms = jnp.exp(masked - row_peak)]
    slice x2 -> x4, local copies, waits for them, and re-layouts: 0.2 us -> 18.5 us  [the longest x2 10.1 us: on_device(): key_heads = pair[0].reshape(seqs, length, HEADS, HEAD_DIM)]
  transfers between devices with their start and end apart: 22 -> 4, of which waited for: 20 -> 3; matrix products, arithmetic and copies ran while one was open for 13% -> 7% of each run, Pallas kernels for 0% -> 0%
where the time goes in v1:
time: 631 us; the launch traced here: 623 us
  Pallas kernels  229 us (36%)
  matrix products  183 us (29%)
  waiting for transfers between devices  75.1 us (12%)
  other arithmetic  70.7 us (11%)
  local copies, waits for them, and re-layouts  57.4 us (9%)
    pallas_call x1, Pallas kernels, gather(): pl.pallas_call(functools.partial(gather_kernel, planes, shapes), out_shap...  115 us
    pallas_call x1, Pallas kernels, scatter_sum(): pl.pallas_call(functools.partial(scatter_kernel, planes, shapes, lags), o...  114 us
    ppermute x1, waiting for transfers between devices, share_keys(): from_x = lax.ppermute(pair, 'ctx', X_SEND)  45.3 us
    convert_element_type x1, other arithmetic, on_device(): d_scores = (attn_probs * (d_probs - jnp.sum(d_probs * attn_probs, axis=-1...  27.7 us
    ppermute x1, waiting for transfers between devices, return_sums(): back = lax.ppermute(chip[0].astype(low), 'ctx', X_BACK)  23.8 us
    dot_general x1, matrix products, on_device(): d_probs = mm('mqhd,mkhd->mhqk', d_context, value_heads)  23 us
    sub x1, matrix products, on_device(): exp_terms = jnp.exp(masked - row_peak)  19.1 us
    dot_general x1, matrix products, on_device(): attended = mm('mhqk,mkhd->mqhd', attn_probs.astype(bf16), value_heads)  16.1 us
  transfers between devices with their start and end apart: 4, of which 3 were waited for; matrix products, arithmetic and copies ran while one was open for 7% of the time, Pallas kernels for 0%

profile of v1, /device:TPU:0, one launch (start us, length us, event | category | flops | bytes accessed | tf_op | source)
XLA Modules:
  0.0 622.7 jit_solution(7311813348802537741)
XLA Ops:
  2.7 115.3 %weight_gather.1 = (bf16[1,4,2,2,2,16,128]{6,5,4,3,2,1,0:T(8,128)(2,1)}, bf16[1,4,2,2,2,32,1024]{6,5,4,3,2,1,0:T(8,128)(2,1)}, bf16[1,4,2,2,2,32,1024]{6,5,4,3,2...) custom-call(bf16[1,16,128]{2,1,0:T(8,128)(2,1)} %copy-done.46, ...), custom_call_target="tpu_custom_call" | custom-call | tf_op jit(solution)/shard_map/weight_gather/pallas_call | solution.py:284
  146.4 45.3 %collective-permute-done = bf16[2,2,256,1024]{3,2,1,0:T(8,128)(2,1)S(1)} collective-permute-done((bf16[2,2,256,1024]{3,2,1,0:T(8,128)(2,1)S(1)}, bf16[2,2,256,1024]{3,2,1,0:T(8,128)(2,1)S(1)}, u32[]{:S(2)}, u32[]{:S(2)}) %collective-permute-start) | collective-permute-done | bytes 2097184 | tf_op jit(solution)/shard_map/ppermute | solution.py:544
  196.0 6.0 collective-permute-done.1
  210.3 6.2 copy.51
  216.5 6.3 %copy.53 = bf16[1,2,1024,1024]{2,3,1,0:T(8,128)(2,1)} copy(bf16[1,2,1024,1024]{3,2,1,0:T(8,128)(2,1)} %get-tuple-element.93) | data formatting | bytes 8388608 | tf_op jit(solution)/shard_map/slice | solution.py:627
  222.9 19.1 %fusion.72 = (f32[2,16,256]{2,1,0:T(8,128)S(1)}, f32[2,16,256,1024]{3,2,1,0:T(8,128)}) fusion(pred[2,256,1024]{2,1,0:T(8,128)(4,1)S(1)} %copy-done.33, bf16[2,1024,16,64]{1,3,2,0:T(8,128)(2,1)} %bitcast.192, bf16[2,256,16,32]{1,3,2,0:T(8,128)(2,1)S(1)} %copy-done.15, bf16[2,256,16,32]{1,3,2,0:T(8,128)(2,1)S(1)} %copy-done.13), kind=kOutput, calls=%fused_computation.154 | convolution fusion | flops 1109394432 | bytes 39354368 | tf_op jit(solution)/shard_map/sub | solution.py:632
  242.0 16.1 %fusion.37 = bf16[2,16,64,256]{3,2,1,0:T(8,128)(2,1)} fusion(bf16[2,1024,16,64]{1,3,2,0:T(8,128)(2,1)} %bitcast.200, f32[2,16,256,1024]{3,2,1,0:T(8,128)} %get-tuple-element.126, f32[2,16,256]{2,1,0:T(8,128)S(1)} %get-tuple-element.125), kind=kOutput, calls=%fused_computation.95 | convolution fusion | flops 1091043328 | bytes 38830080 | tf_op jit(solution)/shard_map/mhqk,mkhd->mqhd/dot_general | solution.py:635
  261.1 8.8 %fusion.73 = f32[2,256,2816]{2,1,0:T(8,128)} fusion(bf16[2,256,1024]{2,1,0:T(8,128)(2,1)S(1)} %multiply_convert_fusion.3, bf16[1024,2816,1]{1,0,2:T(8,128)(2,1)} %bitcast.248), kind=kOutput, calls=%fused_computation.155 | convolution fusion | flops 2952790016 | bytes 12582912 | tf_op jit(solution)/shard_map/ajo,oc->ajc/dot_general | solution.py:640
  275.0 10.4 %fusion.12 = (bf16[2,256,2816]{2,1,0:T(8,128)(2,1)}, bf16[2,256,2816]{2,1,0:T(8,128)(2,1)}, bf16[2,256,2816]{2,1,0:T(8,128)(2,1)}) fusion(f32[2,256,2816]{2,1,0:T(8,128)} %fusion.73, f32[2,256,2816]{2,1,0:T(8,128)} %fusion.74, bf16[2816,1024,1]{1,0,2:T(8,128)(2,1)S(1)} %bitcast.243, bf16[2,256,1024]{2,1,0:T(8,128)(2,1)S(1)} %copy-done.24), kind=kOutput, calls=%fused_computation.31 | convolution fusion | flops 2974416896 | bytes 27000832 | tf_op jit(solution)/shard_map/voc,sc->vos/dot_general | solution.py:647
  285.4 5.1 fusion.75
  298.3 15.0 %fusion.18 = bf16[2,16,64,1024]{3,2,1,0:T(8,128)(2,1)} fusion(bf16[2,256,16,64]{1,3,2,0:T(8,128)(2,1)S(1)} %bitcast.219, f32[2,16,256,1024]{3,2,1,0:T(8,128)} %get-tuple-element.126, f32[2,16,256]{2,1,0:T(8,128)S(1)} %get-tuple-element.125), kind=kOutput, calls=%fused_computation.54 | convolution fusion | flops 1092616192 | bytes 38830080 | tf_op jit(solution)/shard_map/mhqk,mqhd->mkhd/dot_general | solution.py:667
  313.3 23.0 %multiply_reduce_fusion = (f32[2,16,256]{2,1,0:T(8,128)S(1)}, f32[2,16,256,1024]{3,2,1,0:T(8,128)}) fusion(f32[2,16,256,1024]{3,2,1,0:T(8,128)} %get-tuple-element.126, f32[2,16,256]{2,1,0:T(8,128)S(1)} %get-tuple-element.125, bf16[2,256,16,64]{1,3,2,0:T(8,128)(2,1)S(1)} %bitcast.220, bf16[2,1024,16,64]{1,3,2,0:T(8,128)(2,1)} %bitcast.201), kind=kOutput, calls=%fused_computation.2 | convolution fusion | flops 1098899456 | bytes 72417280 | tf_op jit(solution)/shard_map/mqhd,mkhd->mhqk/dot_general | solution.py:666
  336.3 6.2 %copy.59 = bf16[1,2,1024,1024]{3,2,1,0:T(8,128)(2,1)} copy(bf16[1,2,1024,1024]{2,3,1,0:T(8,128)(2,1)} %bitcast.202) | data formatting | bytes 8388608 | tf_op jit(solution)/shard_map/stack;reshape | solution.py:674
  342.6 27.7 %multiply_convert_fusion = bf16[2,16,256,1024]{3,2,1,0:T(8,128)(2,1)} fusion(f32[2,16,256,1024]{3,2,1,0:T(8,128)} %get-tuple-element.131, f32[2,16,256]{2,1,0:T(8,128)S(1)} %get-tuple-element.130, f32[2,16,256,1024]{3,2,1,0:T(8,128)} %get-tuple-element.126, f32[2,16,256]{2,1,0:T(8,128)S(1)} %get-tuple-element.125), kind=kLoop, calls=%fused_computation.1 | loop fusion | flops 33554432 | bytes 83951616 | tf_op jit(solution)/shard_map/convert_element_type | solution.py:670
  370.2 10.8 %multiply_convert_fusion.1 = bf16[2,16,64,1024]{3,2,1,0:T(8,128)(2,1)} fusion(bf16[2,16,256,1024]{3,2,1,0:T(8,128)(2,1)} %multiply_convert_fusion, bf16[2,256,16,32]{1,3,2,0:T(8,128)(2,1)S(1)} %copy-done.16, bf16[2,256,16,32]{1,3,2,0:T(8,128)(2,1)S(1)} %copy-done.14), kind=kOutput, calls=%fused_computation.21 | convolution fusion | flops 1080033280 | bytes 22020096 | tf_op jit(solution)/shard_map/mhqk,mqhd->mkhd/dot_general | solution.py:672
  381.0 6.2 copy.58
  387.2 7.6 %select_bitcast_fusion.2 = (bf16[1,2,2,256,1024]{4,3,2,1,0:T(8,128)(2,1)S(1)}, bf16[2,2,256,1024]{3,2,1,0:T(8,128)(2,1)S(1)}, bf16[1,2,2,256,1024]{4,3,2,1,0:T(8,128)(2,1)S(1)}, bf16[1,2,2,256,1024]{4,3,2,1,0:T(8,128)(2,1)S(1)}) fusion(pred[]{:T(512)S(6)} %eq.24, bf16[1,2,1024,1024]{3,2,1,0:T(8,128)(2,1)} %copy.59, bf16[1,2,1024,1024]{3,2,1,0:T(8,128)(2,1)} %copy.58), kind=kLoop, calls=%fused_computation.80 | loop fusion | flops 28311552 | bytes 16777216 | tf_op jit(solution)/shard_map/stack | solution.py:568
  397.3 5.1 bitcast_convert_fusion.1
  402.5 5.3 bitcast_convert_fusion
  421.5 7.6 %add_convert_fusion = bf16[2,256,1024]{2,1,0:T(8,128)(2,1)} fusion(f32[2,256,1024]{2,1,0:T(8,128)S(1)} %copy-done.6, bf16[2,256,2816]{2,1,0:T(8,128)(2,1)} %get-tuple-element.90, bf16[2816,1024,1]{1,0,2:T(8,128)(2,1)} %bitcast.240), kind=kOutput, calls=%fused_computation.85 | convolution fusion | flops 2953838592 | bytes 11796480 | tf_op jit(solution)/shard_map/biu,ue->bie/dot_general | solution.py:643
  429.1 13.6 %multiply_bitcast_fusion = f32[2,256,16,64]{1,3,2,0:T(8,128)} fusion(bf16[2,1024,16,64]{1,3,2,0:T(8,128)(2,1)} %bitcast.193, bf16[2,16,256,1024]{3,2,1,0:T(8,128)(2,1)} %multiply_convert_fusion), kind=kOutput, calls=%fused_computation.82 | convolution fusion | flops 1074266112 | bytes 23068672 | tf_op jit(solution)/shard_map/mhqk,mkhd->mqhd/dot_general | solution.py:671
  442.7 23.8 %collective-permute-done.3 = bf16[2,2,256,1024]{3,2,1,0:T(8,128)(2,1)} collective-permute-done((bf16[2,2,256,1024]{3,2,1,0:T(8,128)(2,1)}, bf16[2,2,256,1024]{3,2,1,0:T(8,128)(2,1)}, u32[]{:S(2)}, u32[]{:S(2)}) %collective-permute-start.3) | collective-permute-done | bytes 2097184 | tf_op jit(solution)/shard_map/ppermute | solution.py:576
  466.6 5.7 fusion.15
  497.8 114.1 %gradient_scatter.1 = (f32[88,1024]{1,0:T(8,128)}, f32[32,2816]{1,0:T(8,128)}, f32[32,2816]{1,0:T(8,128)}, f32[32,1024]{1,0:T(8,128)}, f32[32,1024]{1,0:T(8,128)...) custom-call(bf16[4,2,2,2,88,1024]{5,4,3,2,1,0:T(8,128)(2,1)} %bitcast.199, ...), custom_call_target="tpu_custom_call" | custom-call | tf_op jit(solution)/shard_map/gradient_scatter/pallas_call | solution.py:505
  (204 shorter events, 110.4 us)
Async XLA Ops:
  119.1 20.8 %copy-start.42 = (f32[1024]{0:T(1024)}, f32[1024]{0:T(1024)S(1)}, u32[]{:S(2)}) copy-start(f32[1024]{0:T(1024)S(1)} %reshape.359) | copy-start | bytes 12292
  121.2 18.7 %copy-start.44 = (f32[2,256]{1,0:T(2,128)}, f32[2,256]{1,0:T(2,128)S(1)}, u32[]{:S(2)}) copy-start(f32[2,256]{1,0:T(2,128)S(1)} %get-tuple-element.122) | copy-start | bytes 6148
  143.2 48.5 %collective-permute-start = (bf16[2,2,256,1024]{3,2,1,0:T(8,128)(2,1)S(1)}, bf16[2,2,256,1024]{3,2,1,0:T(8,128)(2,1)S(1)}, u32[]{:S(2)}, u32[]{:S(2)}) collective-permute-start(bf16[2,2,256,1024]{3,2,1,0:T(8,128)(2,1)S(1)} %get-tuple-element.112), channel_id=1, source_target_pairs={{0,2},{1,3},{4,6},{5,7},{8,10},{9,11},{12,14},{13,15},{16,18},{17,... | collective-permute-start | bytes 6291464 | tf_op jit(solution)/shard_map/ppermute | solution.py:544
  194.4 7.5 %collective-permute-start.1 = (bf16[2,2,2,256,1024]{4,3,2,1,0:T(8,128)(2,1)}, bf16[2,2,2,256,1024]{4,3,2,1,0:T(8,128)(2,1)}, u32[]{:S(2)}, u32[]{:S(2)}) collective-permute-start(bf16[2,2,2,256,1024]{4,3,2,1,0:T(8,128)(2,1)} %pad_maximum_fusion.1), channel_id=1, source_target_pairs={{0,1},{1,0},{2,3},{3,2},{4,5},{5,4},{6,7},{7,6},{8,9},{9,8},{10,11... | collective-permute-start | bytes 12582920 | tf_op jit(solution)/shard_map/ppermute | solution.py:546
  216.5 6.3 %copy-start.33 = (pred[2,256,1024]{2,1,0:T(8,128)(4,1)S(1)}, pred[2,256,1024]{2,1,0:T(8,128)(4,1)}, u32[]{:S(2)}) copy-start(pred[2,256,1024]{2,1,0:T(8,128)(4,1)} %compare_and_fusion) | copy-start | bytes 1572868
  242.0 16.1 %copy-start.21 = (bf16[1,4,2,2,2,32,1024]{6,5,4,3,2,1,0:T(8,128)(2,1)S(1)}, bf16[1,4,2,2,2,32,1024]{6,5,4,3,2,1,0:T(8,128)(2,1)}, u32[]{:S(2)}) copy-start(bf16[1,4,2,2,2,32,1024]{6,5,4,3,2,1,0:T(8,128)(2,1)} %get-tuple-element.68) | copy-start | bytes 6291460
  258.1 11.8 %slice-start.2 = ((s8[5767168]{0:T(1024)(128)(4,1)}), s8[4194304]{0:T(1024)(128)(4,1)S(1)}, s32[]{:S(2)}) async-start(s8[5767168]{0:T(1024)(128)(4,1)} %bitcast.244), calls=%async_computation.2 | async-start | bytes 8388608
  260.8 33.7 %copy-start.5 = (f32[2,256,1024]{2,1,0:T(8,128)}, f32[2,256,1024]{2,1,0:T(8,128)S(1)}, u32[]{:S(2)}) copy-start(f32[2,256,1024]{2,1,0:T(8,128)S(1)} %get-tuple-element.128) | copy-start | bytes 6291460
  261.1 8.8 %copy-start.26 = (bf16[2,256,1024]{2,1,0:T(8,128)(2,1)}, bf16[2,256,1024]{2,1,0:T(8,128)(2,1)S(1)}, u32[]{:S(2)}) copy-start(bf16[2,256,1024]{2,1,0:T(8,128)(2,1)S(1)} %multiply_convert_fusion.3) | copy-start | bytes 3145732
  261.1 8.8 %slice-start.3 = ((s8[5767168]{0:T(1024)(128)(4,1)}), s8[1572864]{0:T(1024)(128)(4,1)S(1)}, s32[]{:S(2)}) async-start(s8[5767168]{0:T(1024)(128)(4,1)} %bitcast.244), calls=%async_computation.3 | async-start | bytes 3145728
  261.1 13.8 %slice-start = ((s8[5767168]{0:T(1024)(128)(4,1)}), s8[4194304]{0:T(1024)(128)(4,1)S(1)}, s32[]{:S(2)}) async-start(s8[5767168]{0:T(1024)(128)(4,1)} %bitcast.241), calls=%async_computation | async-start | bytes 8388608
  269.9 15.4 %slice-start.4 = ((s8[5767168]{0:T(1024)(128)(4,1)}), s8[4194304]{0:T(1024)(128)(4,1)S(1)}, s32[]{:S(2)}) async-start(s8[5767168]{0:T(1024)(128)(4,1)} %bitcast.249), calls=%async_computation.4 | async-start | bytes 8388608
  274.9 10.4 %slice-start.5 = ((s8[5767168]{0:T(1024)(128)(4,1)}), s8[1572864]{0:T(1024)(128)(4,1)S(1)}, s32[]{:S(2)}) async-start(s8[5767168]{0:T(1024)(128)(4,1)} %bitcast.249), calls=%async_computation.5 | async-start | bytes 3145728
  342.5 27.7 %copy-start.14 = (bf16[2,256,16,32]{1,3,2,0:T(8,128)(2,1)S(1)}, bf16[2,256,16,32]{1,3,2,0:T(8,128)(2,1)}, u32[]{:S(2)}) copy-start(bf16[2,256,16,32]{1,3,2,0:T(8,128)(2,1)} %get-tuple-element.107) | copy-start | bytes 1572868
  342.5 27.7 %copy-start.16 = (bf16[2,256,16,32]{1,3,2,0:T(8,128)(2,1)S(1)}, bf16[2,256,16,32]{1,3,2,0:T(8,128)(2,1)}, u32[]{:S(2)}) copy-start(bf16[2,256,16,32]{1,3,2,0:T(8,128)(2,1)} %get-tuple-element.108) | copy-start | bytes 1572868
  387.2 7.7 %copy-start.1 = (bf16[1,2,1024,1024]{3,2,1,0:T(8,128)(2,1)S(1)}, bf16[1,2,1024,1024]{3,2,1,0:T(8,128)(2,1)}, u32[]{:S(2)}) copy-start(bf16[1,2,1024,1024]{3,2,1,0:T(8,128)(2,1)} %copy.59) | copy-start | bytes 12582916
  387.2 7.7 %copy-start.2 = (bf16[1,2,1024,1024]{3,2,1,0:T(8,128)(2,1)S(1)}, bf16[1,2,1024,1024]{3,2,1,0:T(8,128)(2,1)}, u32[]{:S(2)}) copy-start(bf16[1,2,1024,1024]{3,2,1,0:T(8,128)(2,1)} %copy.58) | copy-start | bytes 12582916
  395.6 6.9 %copy-start.51 = (bf16[2,256,2816]{2,1,0:T(8,128)(2,1)S(1)}, bf16[2,256,2816]{2,1,0:T(8,128)(2,1)}, u32[]{:S(2)}) copy-start(bf16[2,256,2816]{2,1,0:T(8,128)(2,1)} %get-tuple-element.88) | copy-start | bytes 8650756
  395.6 17.2 %collective-permute-start.2 = (bf16[2,2,2,256,1024]{4,3,2,1,0:T(8,128)(2,1)S(1)}, bf16[2,2,2,256,1024]{4,3,2,1,0:T(8,128)(2,1)S(1)}, u32[]{:S(2)}, u32[]{:S(2)}) collective-permute-start(bf16[2,2,2,256,1024]{4,3,2,1,0:T(8,128)(2,1)S(1)} %pad_maximum_fusion.2), channel_id=1, source_target_pairs={{0,1},{1,0},{2,3},{3,2},{4,5},{5,4},{6,7},{7,6},{8,9},{9,8},{10,11... | collective-permute-start | bytes 12582920 | tf_op jit(solution)/shard_map/ppermute | solution.py:574
  414.6 6.8 %copy-start = (f32[2,2,2,256,1024]{4,3,2,1,0:T(8,128)}, f32[2,2,2,256,1024]{4,3,2,1,0:T(8,128)S(1)}, u32[]{:S(2)}) copy-start(f32[2,2,2,256,1024]{4,3,2,1,0:T(8,128)S(1)} %convert_add_fusion) | copy-start | bytes 25165828
  416.3 50.3 %collective-permute-start.3 = (bf16[2,2,256,1024]{3,2,1,0:T(8,128)(2,1)}, bf16[2,2,256,1024]{3,2,1,0:T(8,128)(2,1)}, u32[]{:S(2)}, u32[]{:S(2)}) collective-permute-start(bf16[2,2,256,1024]{3,2,1,0:T(8,128)(2,1)} %fusion.21), channel_id=1, source_target_pairs={{2,0},{3,1},{6,4},{7,5},{10,8},{11,9},{14,12},{15,13},{18,16},{19,... | collective-permute-start | bytes 6291464 | tf_op jit(solution)/shard_map/ppermute | solution.py:576
  497.8 115.4 %copy-start.47 = (f32[2,256]{1,0:T(2,128)S(1)}, f32[2,256]{1,0:T(2,128)}, u32[]{:S(2)}) copy-start(f32[2,256]{1,0:T(2,128)} %get-tuple-element.121) | copy-start | bytes 6148
  613.2 6.9 %copy-start.36 = (f32[32,2816]{1,0:T(8,128)S(1)}, f32[32,2816]{1,0:T(8,128)}, u32[]{:S(2)}) copy-start(f32[32,2816]{1,0:T(8,128)} %get-tuple-element.156) | copy-start | bytes 1081348
  613.2 7.6 %copy-start.35 = (f32[32,2816]{1,0:T(8,128)S(1)}, f32[32,2816]{1,0:T(8,128)}, u32[]{:S(2)}) copy-start(f32[32,2816]{1,0:T(8,128)} %get-tuple-element.157) | copy-start | bytes 1081348
  (40 other events, 140.2 us)

commit v2 on v1

--- a/solution.py
+++ b/solution.py
@@ -20,55 +20,320 @@
     return lax.rsqrt(jnp.mean(values * values, axis=-1, keepdims=True) + epsilon)
 
 
-def rotate(values, cos_table, sin_table):
-    half_width = values.shape[-1] // 2
-    first_half = values[..., :half_width]
-    second_half = values[..., half_width:]
-    return jnp.concatenate(
-        [
-            first_half * cos_table - second_half * sin_table,
-            second_half * cos_table + first_half * sin_table,
-        ],
-        axis=-1,
-    )
-
-
-def unrotate(values, cos_table, sin_table):
-    half_width = values.shape[-1] // 2
-    first_half = values[..., :half_width]
-    second_half = values[..., half_width:]
-    return jnp.concatenate(
-        [
-            first_half * cos_table + second_half * sin_table,
-            second_half * cos_table - first_half * sin_table,
-        ],
-        axis=-1,
-    )
-
-
 def swish(values):
     return values * jax.nn.sigmoid(values)
 
 
-def layout(segments, ctx_rank, row_count):
-    length = segments.shape[1]
+def first_half(shape):
+    return lax.broadcasted_iota(jnp.int32, shape, len(shape) - 1) % HEAD_DIM < HEAD_DIM // 2
+
+
+def swap_halves(values):
+    return jnp.where(
+        first_half(values.shape), pltpu.roll(values, 96, 1), pltpu.roll(values, 32, 1)
+    )
+
+
+def turned(values, cos_table, sin_table, sign):
+    return values * cos_table + sign * (swap_halves(values) * sin_table)
+
+
+def tables(segment_ids, rank, rows):
+    seqs, length = segment_ids.shape
     places = jnp.arange(length, dtype=jnp.int32)
-    doc_edges = jnp.concatenate(
-        [jnp.ones((segments.shape[0], 1), dtype=jnp.bool_), segments[:, 1:] != segments[:, :-1]],
+    edges = jnp.concatenate(
+        [jnp.ones((seqs, 1), dtype=jnp.bool_), segment_ids[:, 1:] != segment_ids[:, :-1]], axis=1
+    )
+    starts = lax.cummax(jnp.where(edges, places[None, :], 0), axis=1)
+    starts = lax.dynamic_slice_in_dim(starts, rank * rows, rows, 1)
+    local = rank * rows + jnp.arange(rows, dtype=jnp.int32) - starts
+    lane = jnp.arange(128, dtype=jnp.int32)
+    half = HEAD_DIM // 2
+    frequency = rope_base ** (-(lane % half).astype(jnp.float32) * 2.0 / HEAD_DIM)
+    angles = local.astype(jnp.float32).reshape(seqs * rows, 1) * frequency
+    sign = jnp.where(lane % HEAD_DIM < half, -1.0, 1.0)
+    return starts.reshape(seqs, 1, rows), jnp.cos(angles), jnp.sin(angles) * sign
+
+
+def project_kernel(tok, first, gain, wq, wk, wv, cos_ref, sin_ref, normed, query, pair):
+    f32, bf16 = jnp.float32, jnp.bfloat16
+
+    @pl.when(pl.program_id(0) == 0)
+    def _():
+        values = tok[...].astype(f32)
+        normed[...] = (values * inverse_rms(values) * gain[...].astype(f32)).astype(bf16)
+
+    n1 = normed[...]
+    cos_table, sin_table = cos_ref[...], sin_ref[...]
+    queries = jnp.dot(n1, wq[...], preferred_element_type=f32)
+    keys = jnp.dot(n1, wk[...], preferred_element_type=f32)
+    values = jnp.dot(n1, wv[...], preferred_element_type=f32)
+    for i in range(queries.shape[1] // 128):
+        lanes = slice(i * 128, i * 128 + 128)
+        query[:, lanes] = turned(queries[:, lanes], cos_table, sin_table, 1.0).astype(bf16)
+        pair[0, :, lanes] = turned(keys[:, lanes], cos_table, sin_table, 1.0).astype(bf16)
+    pair[1] = (0.5 * values + 0.5 * first[...].astype(f32)).astype(bf16)
+
+
+def project(tok, first, gain, wq, wk, wv, cos_table, sin_table):
+    rows, width = tok.shape
+    tile = 256
+    whole = lambda i: (0, 0)
+    column = lambda i: (0, i)
+    wide = lambda: pl.BlockSpec((width, tile), column)
+    return pl.pallas_call(
+        project_kernel,
+        grid=(width // tile,),
+        in_specs=[
+            pl.BlockSpec((rows, width), whole),
+            pl.BlockSpec((rows, tile), column),
+            pl.BlockSpec((1, width), whole),
+            wide(),
+            wide(),
+            wide(),
+            pl.BlockSpec((rows, 128), whole),
+            pl.BlockSpec((rows, 128), whole),
+        ],
+        out_specs=[
+            pl.BlockSpec((rows, width), whole),
+            pl.BlockSpec((rows, tile), column),
+            pl.BlockSpec((2, rows, tile), lambda i: (0, 0, i)),
+        ],
+        out_shape=[
+            jax.ShapeDtypeStruct((rows, width), jnp.bfloat16),
+            jax.ShapeDtypeStruct((rows, width), jnp.bfloat16),
+            jax.ShapeDtypeStruct((2, rows, width), jnp.bfloat16),
+        ],
+        name="project",
+    )(tok, first, gain, wq, wk, wv, cos_table, sin_table)
+
+
+def two_heads(block, scale):
+    lane = lax.broadcasted_iota(jnp.int32, block.shape, 1)
+    scaled = block * jnp.asarray(scale, block.dtype)
+    zero = jnp.zeros_like(block)
+    return jnp.concatenate(
+        [jnp.where(lane < HEAD_DIM, scaled, zero), jnp.where(lane < HEAD_DIM, zero, scaled)]
+    )
+
+
+def own_lanes(both):
+    rows = both.shape[1] // 2
+    lane = lax.broadcasted_iota(jnp.int32, (both.shape[0], rows), 0)
+    return jnp.where(lane < HEAD_DIM, both[:, :rows], both[:, rows:]).T
+
+
+def fill_bias(bias, starts, rank):
+    rows = bias.shape[1]
+    key = lax.broadcasted_iota(jnp.int32, (rows, rows), 0)
+    place = rank * rows + lax.broadcasted_iota(jnp.int32, (rows, rows), 1)
+    begin = starts[...]
+    for t in range(4):
+        x, c = lax.div(rank, 2), lax.rem(rank, 2)
+        owner = (1 - x if t >= 2 else x) * 2 + (1 - c if t % 2 else c)
+        at = owner * rows + key
+        bias[t] = jnp.where((at >= begin) & (at <= place), 0.0, masked_score)
+
+
+NT = (((1,), (1,)), ((), ()))
+TN = (((0,), (0,)), ((), ()))
+
+
+def attend_step(rank, begin, starts, q, tiles, out, log_total, bias, scores, peak, total, acc):
+    f32, bf16 = jnp.float32, jnp.bfloat16
+
+    @pl.when(begin)
+    def _():
+        fill_bias(bias, starts, rank)
+
+    high = rank >= 2
+    stacked = two_heads(q, score_scale)
+
+    def score(t):
+        s = lax.dot_general(tiles[t][0][...], stacked, NT, preferred_element_type=f32)
+        s = s + jnp.concatenate([bias[t], bias[t]], axis=1)
+        scores[t] = s
+        return jnp.max(s, axis=0, keepdims=True)
+
+    def gather_values(t, top):
+        e = jnp.exp(scores[t] - top)
+        part = lax.dot_general(tiles[t][1][...], e.astype(bf16), TN, preferred_element_type=f32)
+        return jnp.sum(e, axis=0, keepdims=True), part
+
+    peak[...] = jnp.maximum(score(0), score(1))
+
+    @pl.when(high)
+    def _():
+        peak[...] = jnp.maximum(peak[...], jnp.maximum(score(2), score(3)))
+
+    top = peak[...]
+    sum_a, acc_a = gather_values(0, top)
+    sum_b, acc_b = gather_values(1, top)
+    total[...] = sum_a + sum_b
+    acc[...] = acc_a + acc_b
+
+    @pl.when(high)
+    def _():
+        top = peak[...]
+        sum_a, acc_a = gather_values(2, top)
+        sum_b, acc_b = gather_values(3, top)
+        total[...] += sum_a + sum_b
+        acc[...] += acc_a + acc_b
+
+    out[...] = own_lanes(acc[...] / total[...]).astype(bf16)
+    log_total[...] = peak[...] + jnp.log(total[...])
+
+
+def attend_scratch(rows):
+    return [
+        pltpu.VMEM((4, rows, rows), jnp.float32),
+        pltpu.VMEM((4, rows, 2 * rows), jnp.float32),
+        pltpu.VMEM((1, 2 * rows), jnp.float32),
+        pltpu.VMEM((1, 2 * rows), jnp.float32),
+        pltpu.VMEM((128, 2 * rows), jnp.float32),
+    ]
+
+
+def attend_kernel(starts, q, tile_a, tile_b, tile_c, tile_d, out, log_total, *scratch):
+    attend_step(
+        lax.axis_index("ctx"),
+        pl.program_id(1) == 0,
+        starts.at[0],
+        q[0],
+        [[t.at[0, 0], t.at[1, 0]] for t in (tile_a, tile_b, tile_c, tile_d)],
+        out.at[0],
+        log_total.at[0, 0],
+        *scratch,
+    )
+
+
+def attend(starts, q, tiles):
+    seqs, rows, width = q.shape
+    pairs = width // 128
+    block = lambda: pl.BlockSpec((1, rows, 128), lambda s, p: (s, 0, p))
+    tile = lambda: pl.BlockSpec((2, 1, rows, 128), lambda s, p: (0, s, 0, p))
+    return pl.pallas_call(
+        attend_kernel,
+        grid=(seqs, pairs),
+        in_specs=[
+            pl.BlockSpec((1, 1, rows), lambda s, p: (s, 0, 0)),
+            block(),
+            tile(),
+            tile(),
+            tile(),
+            tile(),
+        ],
+        out_specs=[block(), pl.BlockSpec((1, 1, 1, 2 * rows), lambda s, p: (s, p, 0, 0))],
+        out_shape=[
+            jax.ShapeDtypeStruct(q.shape, jnp.bfloat16),
+            jax.ShapeDtypeStruct((seqs, pairs, 1, 2 * rows), jnp.float32),
+        ],
+        scratch_shapes=attend_scratch(rows),
+        name="attend",
+    )(starts, q, *tiles)
+
+
+def attend_back_step(
+    rank, begin, starts, q, tiles, context, d_context, log_total, cos_t, sin_t, d_q, d_tiles, bias, acc
+):
+    f32, bf16 = jnp.float32, jnp.bfloat16
+
+    @pl.when(begin)
+    def _():
+        fill_bias(bias, starts, rank)
+
+    high = rank >= 2
+    stacked = two_heads(q, score_scale)
+    stacked_do = two_heads(d_context, 1.0)
+    turned_product = (d_context.astype(f32) * context.astype(f32)).T
+    delta = jnp.concatenate(
+        [
+            jnp.sum(turned_product[:HEAD_DIM], axis=0, keepdims=True),
+            jnp.sum(turned_product[HEAD_DIM:], axis=0, keepdims=True),
+        ],
         axis=1,
     )
-    starts = lax.cummax(jnp.where(doc_edges, places[None, :], 0), axis=1)
-    positions = places[None, :] - starts
-    first_row = ctx_rank * row_count
-    local_places = first_row + jnp.arange(row_count, dtype=jnp.int32)
-    local_segments = lax.dynamic_slice_in_dim(segments, first_row, row_count, 1)
-    local_positions = lax.dynamic_slice_in_dim(positions, first_row, row_count, 1)
-    allowed = (local_segments[:, :, None] == segments[:, None, :]) & (
-        places[None, None, :] <= local_places[None, :, None]
-    )
-    frequency = rope_base ** (-jnp.arange(HEAD_DIM // 2, dtype=jnp.float32) * 2.0 / HEAD_DIM)
-    angles = local_positions.astype(jnp.float32)[:, :, None] * frequency
-    return (allowed, jnp.cos(angles)[:, :, None, :], jnp.sin(angles)[:, :, None, :])
+    lse = log_total[...]
+
+    def one(t):
+        keys, values = tiles[t][0][...], tiles[t][1][...]
+        s = lax.dot_general(keys, stacked, NT, preferred_element_type=f32)
+        s = s + jnp.concatenate([bias[t], bias[t]], axis=1)
+        p = jnp.exp(s - lse)
+        dp = lax.dot_general(values, stacked_do, NT, preferred_element_type=f32)
+        ds = (p * (dp - delta)).astype(bf16)
+        d_tiles[t][1][...] = jnp.dot(p.astype(bf16), stacked_do, preferred_element_type=f32).astype(bf16)
+        d_tiles[t][0][...] = jnp.dot(ds, stacked, preferred_element_type=f32).astype(bf16)
+        return lax.dot_general(keys, ds, TN, preferred_element_type=f32)
+
+    acc[...] = one(0) + one(1)
+
+    @pl.when(high)
+    def _():
+        acc[...] += one(2) + one(3)
+
+    d_q[...] = turned(own_lanes(acc[...]) * score_scale, cos_t[...], sin_t[...], -1.0).astype(bf16)
+
+
+def attend_back_scratch(rows):
+    return [pltpu.VMEM((4, rows, rows), jnp.float32), pltpu.VMEM((128, 2 * rows), jnp.float32)]
+
+
+def attend_back_kernel(starts, q, ta, tb, tc, td, o, do, lse, cos_t, sin_t, dq, da, db, dc, dd, *scratch):
+    attend_back_step(
+        lax.axis_index("ctx"),
+        pl.program_id(1) == 0,
+        starts.at[0],
+        q[0],
+        [[t.at[0, 0], t.at[1, 0]] for t in (ta, tb, tc, td)],
+        o[0],
+        do[0],
+        lse.at[0, 0],
+        cos_t.at[0],
+        sin_t.at[0],
+        dq.at[0],
+        [[t.at[0, 0], t.at[1, 0]] for t in (da, db, dc, dd)],
+        *scratch,
+    )
+
+
+def attend_back(starts, q, tiles, context, d_context, log_total, cos_table, sin_table):
+    seqs, rows, width = q.shape
+    pairs = width // 128
+    block = lambda: pl.BlockSpec((1, rows, 128), lambda s, p: (s, 0, p))
+    tile = lambda: pl.BlockSpec((2, 1, rows, 128), lambda s, p: (0, s, 0, p))
+    table = lambda: pl.BlockSpec((1, rows, 128), lambda s, p: (s, 0, 0))
+    return pl.pallas_call(
+        attend_back_kernel,
+        grid=(seqs, pairs),
+        in_specs=[
+            pl.BlockSpec((1, 1, rows), lambda s, p: (s, 0, 0)),
+            block(),
+            tile(),
+            tile(),
+            tile(),
+            tile(),
+            block(),
+            block(),
+            pl.BlockSpec((1, 1, 1, 2 * rows), lambda s, p: (s, p, 0, 0)),
+            table(),
+            table(),
+        ],
+        out_specs=[block(), tile(), tile(), tile(), tile()],
+        out_shape=[jax.ShapeDtypeStruct(q.shape, jnp.bfloat16)]
+        + [jax.ShapeDtypeStruct(tiles[0].shape, jnp.bfloat16)] * 4,
+        scratch_shapes=attend_back_scratch(rows),
+        name="attend_back",
+    )(
+        starts,
+        q,
+        *tiles,
+        context,
+        d_context,
+        log_total,
+        cos_table.reshape(seqs, rows, 128),
+        sin_table.reshape(seqs, rows, 128),
+    )
 
 
 def position():
@@ -122,9 +387,18 @@
     pl.semaphore_wait(barrier, 3 + jnp.where(z > 0, 1, 0) + jnp.where(z < planes - 1, 1, 0))
 
 
-def gather_kernel(planes, shapes, *refs):
+def gather_kernel(planes, shapes, with_pair, *refs):
     n = len(shapes)
-    ins, outs, sems = refs[:n], refs[n : 2 * n], refs[2 * n :]
+    ins, refs = refs[:n], refs[n:]
+    if with_pair:
+        pair, refs = refs[0], refs[1:]
+    outs, refs = refs[:n], refs[n:]
+    if with_pair:
+        tile_b, tile_c, tile_d = refs[:3]
+        refs = refs[3:]
+        pair_send, pair_recv = refs[-2:]
+        refs = refs[:-2]
+    sems = refs
     own_sem, z_send, z_recv, x_send, x_recv, y_send, y_recv, d_send, d_recv, c_send, c_recv = sems
     z, y, x, c = position()
     entry_barrier(z, y, x, c, planes)
@@ -218,6 +492,20 @@
 
         x_copy(g, zz, own).start()
         y_copy(g, zz, own).start()
+
+    if with_pair:
+        to_partner = push(
+            pair, tile_b, pair_send.at[0], pair_recv.at[0], device(z, y, x, 1 - c)
+        )
+        to_x = push(pair, tile_c, pair_send.at[1], pair_recv.at[1], device(z, y, 1 - x, c))
+        passed_on = push(
+            tile_c, tile_d, pair_send.at[2], pair_recv.at[2], device(z, y, x, 1 - c)
+        )
+        to_partner.start()
+
+        @pl.when(x == 0)
+        def _():
+            to_x.start()
 
     items = [(t, g) for t in range(planes) for g in range(n)]
     lag_plane, lag_core = n, 2 * n
@@ -248,6 +536,13 @@
             stage_plane(*items[i - lag_plane])
         if 0 <= i - lag_core < len(items):
             stage_core(*items[i - lag_core])
+    if with_pair:
+
+        @pl.when(x == 1)
+        def _():
+            to_x.wait_recv()
+            passed_on.start()
+
     for t, g in items:
         zz = visit(t, z, planes)
         core_copy(g, zz, False).wait_recv()
@@ -277,18 +572,34 @@
                 z_copy(g, zz, False, False).wait_send()
 
 
-def gather(planes, blocks):
+    if with_pair:
+        to_partner.wait()
+
+        @pl.when(x == 0)
+        def _():
+            to_x.wait_send()
+
+        @pl.when(x == 1)
+        def _():
+            passed_on.wait()
+
+
+def gather(planes, blocks, collective_id, pair=None):
+    blocks = [b[None] for b in blocks]
     n = len(blocks)
     shapes = [b.shape for b in blocks]
     dma = pltpu.SemaphoreType.DMA
-    return pl.pallas_call(
-        functools.partial(gather_kernel, planes, shapes),
+    extra = [] if pair is None else [pair]
+    anywhere = pl.BlockSpec(memory_space=pl.ANY)
+    got = pl.pallas_call(
+        functools.partial(gather_kernel, planes, shapes, pair is not None),
         out_shape=[
             jax.ShapeDtypeStruct((s[0], planes, 2, 2, 2, s[1], s[2]), b.dtype)
             for s, b in zip(shapes, blocks)
-        ],
-        in_specs=[pl.BlockSpec(memory_space=pl.ANY)] * n,
-        out_specs=[pl.BlockSpec(memory_space=pl.ANY)] * n,
+        ]
+        + [jax.ShapeDtypeStruct(p.shape, p.dtype) for p in extra * 3],
+        in_specs=[anywhere] * (n + len(extra)),
+        out_specs=[anywhere] * (n + 3 * len(extra)),
         scratch_shapes=[
             dma((n,)),
             dma((n, planes, 2)),
@@ -301,10 +612,13 @@
             dma((n, planes, 2)),
             dma((n, planes)),
             dma((n, planes)),
-        ],
-        compiler_params=pltpu.CompilerParams(collective_id=0, has_side_effects=True),
+        ]
+        + [dma((3,)), dma((3,))] * len(extra),
+        compiler_params=pltpu.CompilerParams(collective_id=collective_id, has_side_effects=True),
         name="weight_gather",
-    )(*blocks)
+    )(*blocks, *extra)
+    full = [g.reshape(planes * 8 * s[1], s[2]) for g, s in zip(got, shapes)]
+    return full, got[n:]
 
 
 def columns(shape, half):
@@ -312,9 +626,18 @@
     return pl.ds(0, cut) if half == 0 else pl.ds(cut, shape[1] - cut)
 
 
-def scatter_kernel(planes, shapes, lags, *refs):
+def scatter_kernel(planes, shapes, lags, with_tiles, *refs):
     n = len(shapes)
-    parts, outs, refs = refs[:n], refs[n : 2 * n], refs[2 * n :]
+    parts, refs = refs[:n], refs[n:]
+    if with_tiles:
+        d_a, d_b, d_c, d_d, cos_table, sin_table = refs[:6]
+        refs = refs[6:]
+    outs, refs = refs[:n], refs[n:]
+    if with_tiles:
+        d_key, d_value, first_grad = refs[:3]
+        refs = refs[3:]
+        mine, chip, from_b, from_d, back, load_sem, tile_send, tile_recv = refs[-8:]
+        refs = refs[:-8]
     own, from_core, from_dx, from_dy, from_x, from_y, from_z = (
         refs[k * n : (k + 1) * n] for k in range(7)
     )
@@ -334,6 +657,14 @@
             device_id=target,
             device_id_type=MESH_ID,
         )
+
+    f32 = jnp.float32
+
+    def add(dst, *srcs):
+        total = dst[...].astype(f32)
+        for src in srcs:
+            total = total + src[...].astype(f32)
+        dst[...] = total.astype(dst.dtype)
 
     def load(g, zz):
         return pltpu.make_async_copy(
@@ -397,13 +728,38 @@
             device(z, y, x, 1 - c),
         )
 
-    f32 = jnp.float32
-
-    def add(dst, *srcs):
-        total = dst[...].astype(f32)
-        for src in srcs:
-            total = total + src[...].astype(f32)
-        dst[...] = total.astype(dst.dtype)
+    if with_tiles:
+        partner = device(z, y, x, 1 - c)
+        load_mine = pltpu.make_async_copy(d_a, mine, load_sem.at[0])
+        load_chip = pltpu.make_async_copy(d_c, chip, load_sem.at[1])
+        send_b = push(d_b, from_b, tile_send.at[0], tile_recv.at[0], partner)
+        send_d = push(d_d, from_d, tile_send.at[1], tile_recv.at[1], partner)
+        send_back = push(
+            chip, back, tile_send.at[2], tile_recv.at[2], device(z, y, 1 - x, c)
+        )
+        rows = mine.shape[2]
+
+        @pl.when(x == 1)
+        def _():
+            send_d.start()
+            load_chip.start()
+
+        send_b.start()
+        load_mine.start()
+
+        @pl.when(x == 1)
+        def _():
+            load_chip.wait()
+            send_d.wait_recv()
+
+            @pl.loop(0, mine.shape[0] * mine.shape[1] * rows // 32)
+            def _(i):
+                kind = lax.div(i, mine.shape[1] * rows // 32)
+                seq = lax.rem(lax.div(i, rows // 32), mine.shape[1])
+                at = pl.ds(pl.multiple_of(lax.rem(i, rows // 32) * 32, 32), 32)
+                add(chip.at[kind, seq, at], from_d.at[kind, seq, at])
+
+            send_back.start()
 
     for t, g in items:
         zz = visit(t, z, planes)
@@ -486,10 +842,50 @@
         y_copy(g, zz).wait_send()
         if t > 0:
             z_copy(g, zz, True).wait_send()
-
-
-def scatter_sum(planes, partials, lags, collective_id=1):
+    if with_tiles:
+        load_mine.wait()
+        send_b.wait()
+
+        @pl.when(x == 0)
+        def _():
+            send_back.wait_recv()
+
+        @pl.when(x == 1)
+        def _():
+            send_d.wait_send()
+            send_back.wait_send()
+
+        @pl.when(x == 1)
+        def _():
+            back[...] = jnp.zeros_like(back)
+
+        @pl.loop(0, mine.shape[1] * rows // 32)
+        def _(i):
+            seq = lax.div(i, rows // 32)
+            at = pl.ds(pl.multiple_of(lax.rem(i, rows // 32) * 32, 32), 32)
+            flat = pl.ds(pl.multiple_of(i * 32, 32), 32)
+            cos_rows, sin_rows = cos_table[flat, :], sin_table[flat, :]
+            for k in range(mine.shape[3] // 128):
+                lanes = pl.ds(k * 128, 128)
+
+                def summed(kind):
+                    return (
+                        mine[kind, seq, at, lanes].astype(f32)
+                        + from_b[kind, seq, at, lanes].astype(f32)
+                        + back[kind, seq, at, lanes].astype(f32)
+                    )
+
+                d_key[flat, lanes] = turned(summed(0), cos_rows, sin_rows, -1.0).astype(jnp.bfloat16)
+                half = 0.5 * summed(1)
+                d_value[flat, lanes] = half.astype(jnp.bfloat16)
+                first_grad[flat, lanes] = half
+
+
+def scatter_sum(planes, partials, lags, collective_id, tiles=None, angles=None):
     n = len(partials)
+    partials = [
+        p.reshape(planes, 2, 2, 2, p.shape[0] // (planes * 8), p.shape[1]) for p in partials
+    ]
     shapes = [p.shape[4:] for p in partials]
     types = [p.dtype for p in partials]
     dma = pltpu.SemaphoreType.DMA
@@ -502,11 +898,23 @@
             out.append(pltpu.VMEM((*lead, s[0], width), d))
         return out
 
+    extra, extra_out, extra_scratch = [], [], []
+    if tiles is not None:
+        extra = [*tiles, *angles]
+        box = tiles[0].shape
+        flat = (box[1] * box[2], box[3])
+        extra_out = [
+            jax.ShapeDtypeStruct(flat, jnp.bfloat16),
+            jax.ShapeDtypeStruct(flat, jnp.bfloat16),
+            jax.ShapeDtypeStruct(flat, jnp.float32),
+        ]
+        extra_scratch = [pltpu.VMEM(box, jnp.bfloat16)] * 5 + [dma((2,)), dma((3,)), dma((3,))]
     return pl.pallas_call(
-        functools.partial(scatter_kernel, planes, shapes, lags),
-        out_shape=[jax.ShapeDtypeStruct(s, jnp.float32) for s in shapes],
-        in_specs=[pl.BlockSpec(memory_space=pl.ANY)] * n,
-        out_specs=[pl.BlockSpec(memory_space=pltpu.VMEM)] * n,
+        functools.partial(scatter_kernel, planes, shapes, lags, bool(extra)),
+        out_shape=[jax.ShapeDtypeStruct(s, jnp.float32) for s in shapes] + extra_out,
+        in_specs=[pl.BlockSpec(memory_space=pl.ANY)] * (n + len(extra[:4]))
+        + [pl.BlockSpec(memory_space=pltpu.VMEM)] * len(extra[4:]),
+        out_specs=[pl.BlockSpec(memory_space=pltpu.VMEM)] * (n + len(extra_out)),
         scratch_shapes=[
             *boxes((planes, 2, 2)),
             *boxes((planes, 2, 2)),
@@ -526,55 +934,13 @@
             dma((n, planes)),
             dma((n, planes)),
             dma((n, planes + 1)),
+            *extra_scratch,
         ],
         compiler_params=pltpu.CompilerParams(
             collective_id=collective_id, has_side_effects=True, vmem_limit_bytes=62 * 2**20
         ),
         name="gradient_scatter",
-    )(*partials)
-
-
-X_SEND = ((0, 2), (1, 3))
-X_BACK = ((2, 0), (3, 1))
-CORES = ((0, 1), (1, 0), (2, 3), (3, 2))
-
-
-def share_keys(pair):
-    rank = lax.axis_index("ctx")
-    from_x = lax.ppermute(pair, "ctx", X_SEND)
-    both = jnp.stack([pair, from_x])
-    other = lax.ppermute(both, "ctx", CORES)
-    odd = rank % 2 == 1
-    high = rank >= 2
-    first = jnp.where(odd, other, both)
-    second = jnp.where(odd, both, other)
-    zero = jnp.zeros_like(first[0])
-    tiles = [
-        jnp.where(high, first[1], first[0]),
-        jnp.where(high, second[1], second[0]),
-        jnp.where(high, first[0], zero),
-        jnp.where(high, second[0], zero),
-    ]
-    return jnp.concatenate(tiles, axis=2)
-
-
-def return_sums(pair):
-    rank = lax.axis_index("ctx")
-    rows = pair.shape[2] // 4
-    odd = rank % 2 == 1
-    high = rank >= 2
-    tiles = [pair[:, :, i * rows : (i + 1) * rows] for i in range(4)]
-    low = pair.dtype
-    mine = jnp.stack(
-        [jnp.where(odd, tiles[1], tiles[0]), jnp.where(odd, tiles[3], tiles[2])]
-    )
-    theirs = jnp.stack(
-        [jnp.where(odd, tiles[0], tiles[1]), jnp.where(odd, tiles[2], tiles[3])]
-    )
-    got = lax.ppermute(theirs, "ctx", CORES)
-    chip = mine.astype(jnp.float32) + got.astype(jnp.float32)
-    back = lax.ppermute(chip[0].astype(low), "ctx", X_BACK)
-    return jnp.where(high, chip[1], chip[0]) + back.astype(jnp.float32)
+    )(*partials, *extra)
 
 
 def on_device(
@@ -598,60 +964,54 @@
     seqs, rows, width = tokens.shape
     rank = lax.axis_index("ctx")
     share = attn_gain.shape[0]
-    gains = jnp.zeros((1, 16, 128), bf16)
-    gains = gains.at[0, 0, :share].set(attn_gain).at[0, 1, :share].set(ffn_gain)
-    shards = (gains, w_query, w_key, w_value, w_out, gate_weight, up_weight, down_weight)
-    blocks = [s if s.ndim == 3 else s[None] for s in shards]
-    gathered = gather(planes, blocks)
-    gain_all = gathered[0].reshape(devices, 16, 128)
-    attn_gain = gain_all[:, 0, :share].reshape(width)
-    ffn_gain = gain_all[:, 1, :share].reshape(width)
-    w_query, w_key, w_value, w_out, gate_weight, up_weight, down_weight = (
-        g.reshape(devices * b.shape[1], b.shape[2]) for g, b in zip(gathered[1:], blocks[1:])
-    )
-    allowed, cos_table, sin_table = layout(segment_ids, rank, rows)
-
-    head_shape = (seqs, rows, HEADS, HEAD_DIM)
-    mm = functools.partial(jnp.einsum, preferred_element_type=f32)
+    gains = jnp.zeros((16, 128), bf16)
+    gains = gains.at[0, :share].set(attn_gain).at[1, :share].set(ffn_gain)
+    (gains, w_query, w_key, w_value), _ = gather(planes, [gains, w_query, w_key, w_value], 0)
+    gains = gains.reshape(devices, 16, 128)
+    attn_gain = gains[:, 0, :share].reshape(1, width)
+    ffn_gain = gains[:, 1, :share].reshape(1, width)
+    starts, cos_table, sin_table = tables(segment_ids, rank, rows)
+    flat = (seqs * rows, width)
+    local = (seqs, rows, width)
+    tokens = tokens.reshape(flat)
+    mm = functools.partial(jnp.dot, preferred_element_type=f32)
+    by_rows = lambda a, b: lax.dot_general(a, b, TN, preferred_element_type=f32).astype(bf16)
+    back = lambda a, b: lax.dot_general(a, b, NT, preferred_element_type=f32)
+    normed_one, query_rot, pair = project(
+        tokens, first_values.reshape(flat), attn_gain, w_query, w_key, w_value, cos_table, sin_table
+    )
+    query_rot = query_rot.reshape(local)
+    pair = pair.reshape(2, *local)
+    (w_out, gate_weight, up_weight, down_weight, pair), _ = lax.optimization_barrier(
+        ((w_out, gate_weight, up_weight, down_weight, pair), normed_one)
+    )
+    (w_out, gate_weight, up_weight, down_weight), others = gather(
+        planes, [w_out, gate_weight, up_weight, down_weight], 1, pair
+    )
+    tiles = [pair, *others]
+    context3, log_total = attend(starts, query_rot, tiles)
+    context = context3.reshape(flat)
     tokens_float = tokens.astype(f32)
     scale_one = inverse_rms(tokens_float)
-    normed_one = (tokens_float * scale_one * attn_gain.astype(f32)).astype(bf16)
-    queries = mm("mrd,de->mre", normed_one, w_query)
-    keys_lin = mm("mrd,de->mre", normed_one, w_key)
-    values_lin = mm("mrd,de->mre", normed_one, w_value)
-    query_rot = rotate(queries.reshape(head_shape), cos_table, sin_table).astype(bf16)
-    key_rot = rotate(keys_lin.reshape(head_shape), cos_table, sin_table).astype(bf16)
-    values_mixed = (0.5 * values_lin + 0.5 * first_values.astype(f32)).astype(bf16)
-    pair = share_keys(jnp.stack([key_rot.reshape(seqs, rows, width), values_mixed]))
-    length = pair.shape[2]
-    key_heads = pair[0].reshape(seqs, length, HEADS, HEAD_DIM)
-    value_heads = pair[1].reshape(seqs, length, HEADS, HEAD_DIM)
-    scores = mm("mqhd,mkhd->mhqk", query_rot, key_heads) * score_scale
-    masked = jnp.where(allowed[:, None], scores, masked_score)
-    row_peak = jnp.max(masked, axis=-1, keepdims=True)
-    exp_terms = jnp.exp(masked - row_peak)
-    row_total = jnp.sum(exp_terms, axis=-1, keepdims=True)
-    attn_probs = exp_terms / row_total
-    attended = mm("mhqk,mkhd->mqhd", attn_probs.astype(bf16), value_heads)
-    context = attended.astype(bf16).reshape(seqs, rows, width)
-    residual = tokens_float + mm("mrd,de->mre", context, w_out)
+    cotangent = cotangent.reshape(flat)
+    residual = tokens_float + mm(context, w_out)
     scale_two = inverse_rms(residual)
     second_normed = (residual * scale_two * ffn_gain.astype(f32)).astype(bf16)
-    gate = mm("ajo,oc->ajc", second_normed, gate_weight)
-    up = mm("ajo,oc->ajc", second_normed, up_weight)
+    gate = mm(second_normed, gate_weight)
+    up = mm(second_normed, up_weight)
     hidden = (swish(gate) * up).astype(bf16)
-    output = (residual + mm("biu,ue->bie", hidden, down_weight)).astype(bf16)
+    output = (residual + mm(hidden, down_weight)).astype(bf16)
 
     out_float = cotangent.astype(f32)
-    d_down = mm("tba,tby->ay", hidden, cotangent).astype(bf16)
-    d_hidden = mm("voc,sc->vos", cotangent, down_weight)
+    d_down = by_rows(hidden, cotangent)
+    d_hidden = back(cotangent, down_weight)
     sigmoid_gate = jax.nn.sigmoid(gate)
     d_gate = (d_hidden * up * sigmoid_gate * (1.0 + gate * (1.0 - sigmoid_gate))).astype(bf16)
     d_up = (d_hidden * (gate * sigmoid_gate)).astype(bf16)
-    d_gate_weight = mm("noj,noa->ja", second_normed, d_gate).astype(bf16)
-    d_up_weight = mm("noj,noa->ja", second_normed, d_up).astype(bf16)
-    d_normed_two = mm("pvn,zn->pvz", d_gate, gate_weight) + mm("pvn,zn->pvz", d_up, up_weight)
-    d_ffn_gain = jnp.sum(d_normed_two * residual * scale_two, axis=(0, 1))
+    d_gate_weight = by_rows(second_normed, d_gate)
+    d_up_weight = by_rows(second_normed, d_up)
+    d_normed_two = back(d_gate, gate_weight) + back(d_up, up_weight)
+    d_ffn_gain = jnp.sum(d_normed_two * residual * scale_two, axis=0)
     weighted_two = d_normed_two * ffn_gain.astype(f32)
     d_residual = (
         out_float
@@ -661,34 +1021,20 @@
         * jnp.mean(weighted_two * residual, axis=-1, keepdims=True)
     )
     d_residual_low = d_residual.astype(bf16)
-    d_out = mm("mrd,mre->de", context, d_residual_low).astype(bf16)
-    d_context = mm("mre,de->mrd", d_residual_low, w_out).astype(bf16).reshape(head_shape)
-    d_probs = mm("mqhd,mkhd->mhqk", d_context, value_heads)
-    value_part = mm("mhqk,mqhd->mkhd", attn_probs.astype(bf16), d_context)
-    d_scores = (
-        attn_probs * (d_probs - jnp.sum(d_probs * attn_probs, axis=-1, keepdims=True))
-    ).astype(bf16)
-    d_query_rot = mm("mhqk,mkhd->mqhd", d_scores, key_heads) * score_scale
-    key_part = mm("mhqk,mqhd->mkhd", d_scores, query_rot) * score_scale
-    flat = (seqs, length, width)
-    d_pair = return_sums(jnp.stack([key_part.reshape(flat), value_part.reshape(flat)]).astype(bf16))
-    d_key_rot, d_mixed = d_pair[0], d_pair[1]
-    local = (seqs, rows, width)
-    d_query = unrotate(d_query_rot, cos_table, sin_table).astype(bf16).reshape(local)
-    d_key = (
-        unrotate(d_key_rot.reshape(head_shape), cos_table, sin_table).astype(bf16).reshape(local)
-    )
-    d_value = (0.5 * d_mixed).astype(bf16)
-    first_grad = 0.5 * d_mixed
-    d_wq = mm("mrd,mre->de", normed_one, d_query).astype(bf16)
-    d_wk = mm("mrd,mre->de", normed_one, d_key).astype(bf16)
-    d_wv = mm("mrd,mre->de", normed_one, d_value).astype(bf16)
-    d_normed_one = (
-        mm("mre,de->mrd", d_query, w_query)
-        + mm("mre,de->mrd", d_key, w_key)
-        + mm("mre,de->mrd", d_value, w_value)
-    )
-    d_attn_gain = jnp.sum(d_normed_one * tokens_float * scale_one, axis=(0, 1))
+    d_out = by_rows(context, d_residual_low)
+    d_context = back(d_residual_low, w_out).astype(bf16).reshape(local)
+    d_query, *d_tiles = attend_back(
+        starts, query_rot, tiles, context3, d_context, log_total, cos_table, sin_table
+    )
+    d_query = d_query.reshape(flat)
+    s_down, s_gate, s_up, s_out, d_key, d_value, first_grad = scatter_sum(
+        planes, [d_down, d_gate_weight, d_up_weight, d_out], (4, 8), 2, d_tiles, (cos_table, sin_table)
+    )
+    d_wq = by_rows(normed_one, d_query)
+    d_wk = by_rows(normed_one, d_key)
+    d_wv = by_rows(normed_one, d_value)
+    d_normed_one = back(d_query, w_query) + back(d_key, w_key) + back(d_value, w_value)
+    d_attn_gain = jnp.sum(d_normed_one * tokens_float * scale_one, axis=0)
     weighted_one = d_normed_one * attn_gain.astype(f32)
     token_grad = (
         d_residual
@@ -699,15 +1045,13 @@
     )
     d_gains = jnp.stack([d_attn_gain, d_ffn_gain]).reshape(2, devices, share)
     d_gains = jnp.zeros((devices, 8, 256), f32).at[:, :2, :share].set(d_gains.transpose(1, 0, 2))
-    partials = [
-        g.reshape(planes, 2, 2, 2, g.size // g.shape[-1] // devices, g.shape[-1])
-        for g in (d_down, d_gate_weight, d_up_weight, d_out, d_wq, d_wk, d_wv, d_gains)
-    ]
-    s_down, s_gate, s_up, s_out, s_wq, s_wk, s_wv, s_gains = scatter_sum(planes, partials, (4, 8))
+    s_wq, s_wk, s_wv, s_gains = scatter_sum(
+        planes, [d_wq, d_wk, d_wv, d_gains.reshape(devices * 8, 256)], (4, 8), 3
+    )
     return (
-        output,
-        token_grad,
-        first_grad,
+        output.reshape(local),
+        token_grad.reshape(local),
+        first_grad.reshape(local),
         s_gains[0, :share],
         s_wq,
         s_wk,

time: 631 us -> 534 us (0.85)
  Pallas kernels: 229 us -> 412 us
  matrix products: 183 us -> 89.4 us
  waiting for transfers between devices: 75.1 us -> 0 us
  other arithmetic: 70.7 us -> 13.5 us
  local copies, waits for them, and re-layouts: 57.4 us -> 13.9 us
    pallas_call x2 -> x7, Pallas kernels: 229 us -> 412 us  [the longest x2 199 us: scatter_sum(): pl.pallas_call(functools.partial(scatter_kernel, planes, shapes, lags, bo...]
    ppermute x4 -> x0, waiting for transfers between devices: 75.1 us -> none  [the longest x1 45.3 us: share_keys(): from_x = lax.ppermute(pair, 'ctx', X_SEND)]
    dot_general x26 -> x18, matrix products: 164 us -> 89.4 us  [the longest x7 35.3 us: on_device(): back = lambda a, b: lax.dot_general(a, b, NT, preferred_element_type=f32)]
    convert_element_type x4 -> x1, other arithmetic: 27.8 us -> 0.01 us  [tables(): angles = local.astype(jnp.float32).reshape(seqs * rows, 1) * frequency]
    sub x1 -> x0, matrix products: 19.1 us -> none  [on_device(): exp_terms = jnp.exp(masked - row_peak)]
    slice x4 -> x1, local copies, waits for them, and re-layouts: 18.5 us -> 0.85 us  [on_device(): attn_gain = gains[:, 0, :share].reshape(1, width)]
    another operation x9 -> x3, other arithmetic: 15.1 us -> 0.81 us  [the longest x1 7.65 us: return_sums(): jnp.stack([jnp.where(odd, tiles[1], tiles[0]), jnp.where(odd, tiles[3], t...]
    another operation x3 -> x2, local copies, waits for them, and re-layouts: 12.6 us -> 0.89 us  [the longest x1 0.68 us: on_device(): attn_gain = gains[:, 0, :share].reshape(1, width)]
  transfers between devices with their start and end apart: 4 -> 0, of which waited for: 3 -> 0; matrix products, arithmetic and copies ran while one was open for 7% -> 0% of each run, Pallas kernels for 0% -> 0%
where the time goes in v2:
time: 534 us; the launch traced here: 530 us
  Pallas kernels  412 us (77%)
  matrix products  89.4 us (17%)
  local copies, waits for them, and re-layouts  13.9 us (3%)
  other arithmetic  13.5 us (3%)
    pallas_call x2, Pallas kernels, scatter_sum(): pl.pallas_call(functools.partial(scatter_kernel, planes, shapes, lags, bo...  199 us
    pallas_call x2, Pallas kernels, gather(): pl.pallas_call(functools.partial(gather_kernel, planes, shapes, pair is n...  164 us
    dot_general x7, matrix products, on_device(): back = lambda a, b: lax.dot_general(a, b, NT, preferred_element_type=f32)  35.3 us
    dot_general x7, matrix products, on_device(): lax.dot_general(a, b, TN, preferred_element_type=f32).astype(bf16)  29.7 us
    pallas_call x1, Pallas kernels, attend_back(): pl.pallas_call(attend_back_kernel, grid=(seqs, pairs), in_specs=[pl.Block...  21.9 us
    pallas_call x1, Pallas kernels, attend(): pl.pallas_call(attend_kernel, grid=(seqs, pairs), in_specs=[pl.BlockSpec(...  17.6 us

profile of v2, /device:TPU:0, one launch (start us, length us, event | category | flops | bytes accessed | tf_op | source)
XLA Modules:
  0.0 529.7 jit_solution(9627018457942238055)
XLA Ops:
  6.6 37.0 %weight_gather.2 = (bf16[1,4,2,2,2,16,128]{6,5,4,3,2,1,0:T(8,128)(2,1)}, bf16[1,4,2,2,2,32,1024]{6,5,4,3,2,1,0:T(8,128)(2,1)}, bf16[1,4,2,2,2,32,1024]{6,5,4,3,2...) custom-call(bf16[1,16,128]{2,1,0:T(8,128)(2,1)} %copy-done.17, bf16[1,32,1024]{2,1,0:T(8,128)(2,1)} %bitcast.145, ...), custom_call_target="tpu_custom_call" | custom-call | tf_op jit(solution)/shard_map/weight_gather/pallas_call | solution.py:594
  45.1 8.7 %project.1 = (bf16[512,1024]{1,0:T(8,128)(2,1)}, bf16[512,1024]{1,0:T(8,128)(2,1)}, bf16[2,512,1024]{2,1,0:T(8,128)(2,1)}) custom-call(bf16[512,1024]{1,0:T(8,128)(2,1)} %bitcast.116, bf16[512,1024]{1,0:T(8,128)(2,1)} %bitcast.141, bf16[1,1024]{1,0:T(2,128)(2,1)} %reshape_squeeze.4.gain, bf16[1024,1024]{1,0:T(8,128)(2,1)} %bitcast.131, ...), custom_call_target="tpu_custom_call" | custom-call | tf_op jit(solution)/shard_map/project/pallas_call | solution.py:84
  53.8 127.0 %weight_gather.3 = (bf16[1,4,2,2,2,32,1024]{6,5,4,3,2,1,0:T(8,128)(2,1)}, bf16[1,4,2,2,2,32,2816]{6,5,4,3,2,1,0:T(8,128)(2,1)}, bf16[1,4,2,2,2,32,2816]{6,5,4,3,...) custom-call(bf16[1,32,1024]{2,1,0:T(8,128)(2,1)} %bitcast.148, ...), custom_call_target="tpu_custom_call" | custom-call | tf_op jit(solution)/shard_map/weight_gather/pallas_call | solution.py:594
  181.3 17.6 %attend.1 = (bf16[2,256,1024]{2,1,0:T(8,128)(2,1)}, f32[2,8,1,512]{3,2,1,0:T(1,128)}) custom-call(s32[2,1,256]{2,1,0:T(1,128)} %reshape.337.starts, bf16[2,256,1024]{2,1,0:T(8,128)(2,1)} %bitcast.123, bf16[2,2,256,1024]{3,2,1,0:T(8,128)(2,1)} %bitcast.114, bf16[2,2,256,1024]{3,2,1,0:T(8,128)(2,1)} %get-tuple-element.97.tile_b.tb, ...), custom_call_target="tpu_custom_call" | custom-call | tf_op jit(solution)/shard_map/attend/pallas_call | solution.py:215
  198.9 4.6 multiply_reduce_fusion.3
  206.5 8.0 %fusion.21 = f32[512,2816]{1,0:T(8,128)} fusion(bf16[512,1024]{1,0:T(8,128)(2,1)S(1)} %multiply_convert_fusion.1, bf16[1024,2816]{1,0:T(8,128)(2,1)} %bitcast.165), kind=kOutput, calls=%fused_computation.73 | convolution fusion | flops 2952790016 | bytes 12582912 | tf_op jit(solution)/shard_map/dot_general | solution.py:1001
  214.6 4.9 fusion.20
  219.5 10.2 %fusion.3 = (bf16[512,2816]{1,0:T(8,128)(2,1)S(1)}, bf16[512,2816]{1,0:T(8,128)(2,1)}, bf16[512,2816]{1,0:T(8,128)(2,1)}) fusion(f32[512,2816]{1,0:T(8,128)} %fusion.20, f32[512,2816]{1,0:T(8,128)} %fusion.21, bf16[2816,1024]{1,0:T(8,128)(2,1)S(1)} %bitcast.164, bf16[512,1024]{1,0:T(8,128)(2,1)S(1)} %bitcast.135), kind=kOutput, calls=%fused_computation.5 | convolution fusion | flops 2974416896 | bytes 27000832 | tf_op jit(solution)/shard_map/dot_general | solution.py:979
  229.7 6.1 %fusion.22 = f32[512,1024]{1,0:T(8,128)S(1)} fusion(bf16[512,2816]{1,0:T(8,128)(2,1)} %get-tuple-element.129, bf16[1024,2816]{1,0:T(8,128)(2,1)S(1)} %bitcast.172), kind=kOutput, calls=%fused_computation.74 | convolution fusion | flops 2952790016 | bytes 10747904 | tf_op jit(solution)/shard_map/dot_general | solution.py:979
  235.9 3.5 multiply_reduce_fusion
  245.1 21.9 %attend_back.1 = (bf16[2,256,1024]{2,1,0:T(8,128)(2,1)}, bf16[2,2,256,1024]{3,2,1,0:T(8,128)(2,1)}, bf16[2,2,256,1024]{3,2,1,0:T(8,128)(2,1)}, bf16[2,2,256,1024...) custom-call(s32[2,1,256]{2,1,0:T(1,128)} %reshape.337.starts, bf16[2,256,1024]{2,1,0:T(8,128)(2,1)} %bitcast.124, ...), custom_call_target="tpu_custom_call" | custom-call | tf_op jit(solution)/shard_map/attend_back/pallas_call | solution.py:306
  267.0 4.7 convolution_convert_fusion.6
  271.6 5.0 convolution_convert_fusion
  276.7 5.5 %convolution_convert_fusion.1 = bf16[1024,2816]{1,0:T(8,128)(2,1)} fusion(bf16[512,1024]{1,0:T(8,128)(2,1)S(1)} %copy-done.8, bf16[512,2816]{1,0:T(8,128)(2,1)S(1)} %copy-done.26), kind=kOutput, calls=%fused_computation.10 | convolution fusion | flops 2955673600 | bytes 9699328 | tf_op jit(solution)/shard_map/dot_general | solution.py:978
  282.2 5.0 convolution_convert_fusion.2
  287.2 165.6 %gradient_scatter.2 = (f32[88,1024]{1,0:T(8,128)}, f32[32,2816]{1,0:T(8,128)}, f32[32,2816]{1,0:T(8,128)}, f32[32,1024]{1,0:T(8,128)}, bf16[512,1024]{1,0:T(8,12...) custom-call(bf16[4,2,2,2,88,1024]{5,4,3,2,1,0:T(8,128)(2,1)} %bitcast.122, ...), custom_call_target="tpu_custom_call" | custom-call | tf_op jit(solution)/shard_map/gradient_scatter/pallas_call | solution.py:912
  452.8 4.7 fusion.24
  457.5 2.6 fusion.23
  460.5 5.9 %fusion.9 = (f32[1024]{0:T(1024)S(1)}, f32[512]{0:T(512)S(1)}, f32[512,1024]{1,0:T(8,128)}) fusion(f32[512]{0:T(512)S(1)} %bitcast.150, bf16[2,256,1024]{2,1,0:T(8,128)(2,1)S(1)} %copy-done, f32[1024]{0:T(1024)S(1)} %reshape.364, bf16[512,1024]{1,0:T(8,128)(2,1)S(1)} %copy-done.9, bf16[1024,1024]{1,0:T(8,128)(2,1)} %bitcast.119, f32[512,1024]{1,0:T(8,128)} %fusion.23, ...), kind=kOutput, calls=%fused_computation.20 | convolution fusion | flops 1078458880 | bytes 10498048 | tf_op jit(solution)/shard_map/dot_general | solution.py:979
  467.3 4.3 convolution_convert_fusion.4
  471.6 2.7 convolution_convert_fusion.3
  476.9 33.9 %gradient_scatter.3 = (f32[32,1024]{1,0:T(8,128)}, f32[32,1024]{1,0:T(8,128)}, f32[32,1024]{1,0:T(8,128)}, f32[8,256]{1,0:T(8,128)}) custom-call(bf16[4,2,2,2,32,1024]{5,4,3,2,1,0:T(8,128)(2,1)} %bitcast.129, bf16[4,2,2,2,32,1024]{5,4,3,2,1,0:T(8,128)(2,1)} %bitcast.127, bf16[4,2,2,2,32,1024]{5,4,3,2,1,0:T(8,128)(2,1)} %bitcast.128, ...), custom_call_target="tpu_custom_call" | custom-call | tf_op jit(solution)/shard_map/gradient_scatter/pallas_call | solution.py:912
  512.1 4.3 fusion.6
  516.3 6.9 %add_convert_fusion = bf16[512,1024]{1,0:T(8,128)(2,1)} fusion(f32[512,1024]{1,0:T(8,128)S(1)} %copy-done.3, bf16[512,2816]{1,0:T(8,128)(2,1)S(1)} %copy-done.25, bf16[2816,1024]{1,0:T(8,128)(2,1)} %bitcast.161), kind=kOutput, calls=%fused_computation.26 | convolution fusion | flops 2953838592 | bytes 11796480 | tf_op jit(solution)/shard_map/dot_general | solution.py:1003
  (116 shorter events, 28.0 us)
Async XLA Ops:
  181.3 17.6 %copy-start = (bf16[2,256,1024]{2,1,0:T(8,128)(2,1)S(1)}, bf16[2,256,1024]{2,1,0:T(8,128)(2,1)}, u32[]{:S(2)}) copy-start(bf16[2,256,1024]{2,1,0:T(8,128)(2,1)} %param.19) | copy-start | bytes 3145732
  204.5 10.0 %slice-start.4 = ((s8[5767168]{0:T(1024)(128)(4,1)}), s8[4194304]{0:T(1024)(128)(4,1)S(1)}, s32[]{:S(2)}) async-start(s8[5767168]{0:T(1024)(128)(4,1)} %bitcast.169), calls=%async_computation.4 | async-start | bytes 8388608
  206.5 8.1 %copy-start.7 = (bf16[512,1024]{1,0:T(8,128)(2,1)}, bf16[512,1024]{1,0:T(8,128)(2,1)S(1)}, u32[]{:S(2)}) copy-start(bf16[512,1024]{1,0:T(8,128)(2,1)S(1)} %multiply_convert_fusion.1) | copy-start | bytes 3145732
  206.5 8.1 %slice-start.5 = ((s8[5767168]{0:T(1024)(128)(4,1)}), s8[1572864]{0:T(1024)(128)(4,1)S(1)}, s32[]{:S(2)}) async-start(s8[5767168]{0:T(1024)(128)(4,1)} %bitcast.169), calls=%async_computation.5 | async-start | bytes 3145728
  206.5 13.0 %slice-start = ((s8[5767168]{0:T(1024)(128)(4,1)}), s8[4194304]{0:T(1024)(128)(4,1)S(1)}, s32[]{:S(2)}) async-start(s8[5767168]{0:T(1024)(128)(4,1)} %bitcast.162), calls=%async_computation | async-start | bytes 8388608
  214.5 4.9 copy-start.6
  214.6 4.9 slice-start.1
  214.6 21.3 %slice-start.2 = ((s8[5767168]{0:T(1024)(128)(4,1)}), s8[4194304]{0:T(1024)(128)(4,1)S(1)}, s32[]{:S(2)}) async-start(s8[5767168]{0:T(1024)(128)(4,1)} %bitcast.166), calls=%async_computation.2 | async-start | bytes 8388608
  219.5 16.3 %slice-start.3 = ((s8[5767168]{0:T(1024)(128)(4,1)}), s8[1572864]{0:T(1024)(128)(4,1)S(1)}, s32[]{:S(2)}) async-start(s8[5767168]{0:T(1024)(128)(4,1)} %bitcast.166), calls=%async_computation.3 | async-start | bytes 3145728
  229.7 6.1 %copy-start.22 = (bf16[512,2816]{1,0:T(8,128)(2,1)}, bf16[512,2816]{1,0:T(8,128)(2,1)S(1)}, u32[]{:S(2)}) copy-start(bf16[512,2816]{1,0:T(8,128)(2,1)S(1)} %get-tuple-element.128) | copy-start | bytes 8650756
  229.7 6.1 %copy-start.2 = (f32[512,1024]{1,0:T(8,128)S(1)}, f32[512,1024]{1,0:T(8,128)}, u32[]{:S(2)}) copy-start(f32[512,1024]{1,0:T(8,128)} %get-tuple-element.140) | copy-start | bytes 6291460
  266.9 4.7 copy-start.8
  266.9 4.7 copy-start.23
  271.6 5.1 copy-start.26
  276.7 5.5 %copy-start.24 = (bf16[512,2816]{1,0:T(8,128)(2,1)S(1)}, bf16[512,2816]{1,0:T(8,128)(2,1)}, u32[]{:S(2)}) copy-start(bf16[512,2816]{1,0:T(8,128)(2,1)} %get-tuple-element.130) | copy-start | bytes 8650756
  452.8 4.7 copy-start.5
  452.8 4.7 copy-start.20
  467.3 4.3 copy-start.19
  512.0 4.3 copy-start.3
  512.0 4.3 copy-start.25
  516.3 6.9 %copy-start.4 = (f32[512,1024]{1,0:T(8,128)S(1)}, f32[512,1024]{1,0:T(8,128)}, u32[]{:S(2)}) copy-start(f32[512,1024]{1,0:T(8,128)} %get-tuple-element.113) | copy-start | bytes 6291460
  523.2 4.0 copy-start.12
  523.3 4.7 copy-start.11
  524.6 4.1 copy-start.10
  (9 other events, 19.6 us)

commit v3 on v2

--- a/solution.py
+++ b/solution.py
@@ -279,63 +279,6 @@
     return [pltpu.VMEM((4, rows, rows), jnp.float32), pltpu.VMEM((128, 2 * rows), jnp.float32)]
 
 
-def attend_back_kernel(starts, q, ta, tb, tc, td, o, do, lse, cos_t, sin_t, dq, da, db, dc, dd, *scratch):
-    attend_back_step(
-        lax.axis_index("ctx"),
-        pl.program_id(1) == 0,
-        starts.at[0],
-        q[0],
-        [[t.at[0, 0], t.at[1, 0]] for t in (ta, tb, tc, td)],
-        o[0],
-        do[0],
-        lse.at[0, 0],
-        cos_t.at[0],
-        sin_t.at[0],
-        dq.at[0],
-        [[t.at[0, 0], t.at[1, 0]] for t in (da, db, dc, dd)],
-        *scratch,
-    )
-
-
-def attend_back(starts, q, tiles, context, d_context, log_total, cos_table, sin_table):
-    seqs, rows, width = q.shape
-    pairs = width // 128
-    block = lambda: pl.BlockSpec((1, rows, 128), lambda s, p: (s, 0, p))
-    tile = lambda: pl.BlockSpec((2, 1, rows, 128), lambda s, p: (0, s, 0, p))
-    table = lambda: pl.BlockSpec((1, rows, 128), lambda s, p: (s, 0, 0))
-    return pl.pallas_call(
-        attend_back_kernel,
-        grid=(seqs, pairs),
-        in_specs=[
-            pl.BlockSpec((1, 1, rows), lambda s, p: (s, 0, 0)),
-            block(),
-            tile(),
-            tile(),
-            tile(),
-            tile(),
-            block(),
-            block(),
-            pl.BlockSpec((1, 1, 1, 2 * rows), lambda s, p: (s, p, 0, 0)),
-            table(),
-            table(),
-        ],
-        out_specs=[block(), tile(), tile(), tile(), tile()],
-        out_shape=[jax.ShapeDtypeStruct(q.shape, jnp.bfloat16)]
-        + [jax.ShapeDtypeStruct(tiles[0].shape, jnp.bfloat16)] * 4,
-        scratch_shapes=attend_back_scratch(rows),
-        name="attend_back",
-    )(
-        starts,
-        q,
-        *tiles,
-        context,
-        d_context,
-        log_total,
-        cos_table.reshape(seqs, rows, 128),
-        sin_table.reshape(seqs, rows, 128),
-    )
-
-
 def position():
     dp = lax.axis_index("dp")
     ct = lax.axis_index("ctx")
@@ -626,18 +569,18 @@
     return pl.ds(0, cut) if half == 0 else pl.ds(cut, shape[1] - cut)
 
 
-def scatter_kernel(planes, shapes, lags, with_tiles, *refs):
+def scatter_kernel(planes, shapes, with_tiles, *refs):
     n = len(shapes)
     parts, refs = refs[:n], refs[n:]
     if with_tiles:
-        d_a, d_b, d_c, d_d, cos_table, sin_table = refs[:6]
-        refs = refs[6:]
+        starts, query, *tiles, context, d_context, log_total, cos_table, sin_table = refs[:11]
+        refs = refs[11:]
     outs, refs = refs[:n], refs[n:]
     if with_tiles:
-        d_key, d_value, first_grad = refs[:3]
-        refs = refs[3:]
-        mine, chip, from_b, from_d, back, load_sem, tile_send, tile_recv = refs[-8:]
-        refs = refs[:-8]
+        d_query, d_key, d_value, first_grad = refs[:4]
+        refs = refs[4:]
+        mine, near, chip, far, from_b, from_d, tile_send, tile_recv, bias, acc = refs[-10:]
+        refs = refs[:-10]
     own, from_core, from_dx, from_dy, from_x, from_y, from_z = (
         refs[k * n : (k + 1) * n] for k in range(7)
     )
@@ -646,7 +589,6 @@
     ]
     z, y, x, c = position()
     entry_barrier(z, y, x, c, planes)
-    items = [(planes - 1 - t, g) for t in range(planes) for g in range(n)]
 
     def push(src, dst, send, recv, target):
         return pltpu.make_async_remote_copy(
@@ -680,15 +622,23 @@
             device(z, y, x, 1 - c),
         )
 
-    def diag(g, zz, half):
-        part = columns(shapes[g], half)
-        box = (from_dx if half == 0 else from_dy)[g].at[zz]
+    def diag_x(g, zz):
+        return push(
+            own[g].at[zz, 1 - y, 1 - x, :, columns(shapes[g], 0)],
+            from_dx[g].at[zz],
+            d_send.at[g, zz, 0],
+            d_recv.at[g, zz, 0],
+            device(z, y, 1 - x, c),
+        )
+
+    def diag_y(g, zz, full):
+        part = slice(None) if full else columns(shapes[g], 1)
         return push(
             own[g].at[zz, 1 - y, 1 - x, :, part],
-            box,
-            d_send.at[g, zz, half],
-            d_recv.at[g, zz, half],
-            device(z, y, 1 - x, c) if half == 0 else device(z, 1 - y, x, c),
+            from_dy[g].at[zz, :, part],
+            d_send.at[g, zz, 1],
+            d_recv.at[g, zz, 1],
+            device(z, 1 - y, x, c),
         )
 
     def x_copy(g, zz):
@@ -728,70 +678,154 @@
             device(z, y, x, 1 - c),
         )
 
+    def lean_or_even(lean, even):
+        if not with_tiles:
+            even()
+            return
+        pl.when(x == 0)(even)
+        pl.when(x == 1)(lean)
+
     if with_tiles:
         partner = device(z, y, x, 1 - c)
-        load_mine = pltpu.make_async_copy(d_a, mine, load_sem.at[0])
-        load_chip = pltpu.make_async_copy(d_c, chip, load_sem.at[1])
-        send_b = push(d_b, from_b, tile_send.at[0], tile_recv.at[0], partner)
-        send_d = push(d_d, from_d, tile_send.at[1], tile_recv.at[1], partner)
-        send_back = push(
-            chip, back, tile_send.at[2], tile_recv.at[2], device(z, y, 1 - x, c)
-        )
-        rows = mine.shape[2]
-
-        @pl.when(x == 1)
-        def _():
-            send_d.start()
-            load_chip.start()
-
-        send_b.start()
-        load_mine.start()
-
-        @pl.when(x == 1)
-        def _():
-            load_chip.wait()
-            send_d.wait_recv()
-
-            @pl.loop(0, mine.shape[0] * mine.shape[1] * rows // 32)
-            def _(i):
-                kind = lax.div(i, mine.shape[1] * rows // 32)
-                seq = lax.rem(lax.div(i, rows // 32), mine.shape[1])
-                at = pl.ds(pl.multiple_of(lax.rem(i, rows // 32) * 32, 32), 32)
-                add(chip.at[kind, seq, at], from_d.at[kind, seq, at])
-
-            send_back.start()
-
-    for t, g in items:
-        zz = visit(t, z, planes)
-        core_copy(g, zz).start()
-        load(g, zz).start()
-
-    def stage_core(t, g):
+        seqs, rows = mine.shape[1:3]
+        pairs = mine.shape[3] // 128
+
+        def send_b(s):
+            return push(
+                near.at[:, s], from_b.at[:, s], tile_send.at[0, s], tile_recv.at[0, s], partner
+            )
+
+        def send_d(s):
+            return push(
+                far.at[:, s], from_d.at[:, s], tile_send.at[1, s], tile_recv.at[1, s], partner
+            )
+
+        def send_back(s):
+            return push(
+                chip.at[:, s],
+                chip.at[:, s],
+                tile_send.at[2, s],
+                tile_recv.at[2, s],
+                device(z, y, 1 - x, c),
+            )
+
+        def unit(u):
+            s, p = lax.div(u, pairs), lax.rem(u, pairs)
+            lanes = pl.ds(pl.multiple_of(p * 128, 128), 128)
+            flat = pl.ds(pl.multiple_of(s * rows, rows), rows)
+            two = lambda ref: [ref.at[0, s, :, lanes], ref.at[1, s, :, lanes]]
+            attend_back_step(
+                lax.axis_index("ctx"),
+                p == 0,
+                starts.at[s],
+                query[s, :, lanes],
+                [two(t) for t in tiles],
+                context[s, :, lanes],
+                d_context[s, :, lanes],
+                log_total.at[s, p],
+                cos_table.at[flat],
+                sin_table.at[flat],
+                d_query.at[s, :, lanes],
+                [two(t) for t in (mine, near, chip, far)],
+                bias,
+                acc,
+            )
+
+        def work(i):
+            each = seqs * pairs // 4
+
+            @pl.when(i < 4)
+            def _():
+                @pl.loop(0, each)
+                def _(j):
+                    unit(i * each + j)
+
+            @pl.when((i == 1) | (i == 3))
+            def _():
+                s = lax.div(i, 2)
+                send_b(s).start()
+
+                @pl.when(x == 1)
+                def _():
+                    send_d(s).start()
+
+            @pl.when(((i == 2) | (i == 4)) & (x == 1))
+            def _():
+                s = lax.div(i, 2) - 1
+                send_d(s).wait_recv()
+                for kind in range(2):
+
+                    @pl.loop(0, rows // 32)
+                    def _(j):
+                        at = pl.ds(pl.multiple_of(j * 32, 32), 32)
+                        add(chip.at[kind, s, at], from_d.at[kind, s, at])
+
+                send_back(s).start()
+
+    @pl.loop(0, planes)
+    def _(r):
+        zz = visit(planes - 1 - r, z, planes)
+        for g in range(n):
+            core_copy(g, zz).start()
+            load(g, zz).start()
+
+    def stage_core(g, t):
         zz = visit(t, z, planes)
         load(g, zz).wait()
         core_copy(g, zz).wait_recv()
         add(own[g].at[zz, 1 - y, 1 - x], from_core[g].at[zz, 1 - y, 1 - x])
-        diag(g, zz, 0).start()
-        diag(g, zz, 1).start()
+
+        def even():
+            diag_x(g, zz).start()
+            diag_y(g, zz, False).start()
+
+        lean_or_even(lambda: diag_y(g, zz, True).start(), even)
+        add(own[g].at[zz, 1 - y, x], from_core[g].at[zz, 1 - y, x])
+        if with_tiles:
+
+            @pl.when(x == 0)
+            def _():
+                y_copy(g, zz).start()
+
         add(own[g].at[zz, y, 1 - x], from_core[g].at[zz, y, 1 - x])
-        add(own[g].at[zz, 1 - y, x], from_core[g].at[zz, 1 - y, x])
         add(own[g].at[zz, y, x], from_core[g].at[zz, y, x])
 
-    def stage_plane(t, g):
+    def stage_plane(g, t):
         zz = visit(t, z, planes)
-        diag(g, zz, 0).wait_recv()
-        add(own[g].at[zz, 1 - y, x, :, columns(shapes[g], 0)], from_dx[g].at[zz])
-        y_copy(g, zz).start()
-        diag(g, zz, 1).wait_recv()
-        add(own[g].at[zz, y, 1 - x, :, columns(shapes[g], 1)], from_dy[g].at[zz])
-        x_copy(g, zz).start()
-
-    def stage_line(t, g):
+
+        def take_x():
+            diag_x(g, zz).wait_recv()
+            add(own[g].at[zz, 1 - y, x, :, columns(shapes[g], 0)], from_dx[g].at[zz])
+            y_copy(g, zz).start()
+
+        def take_y(full):
+            part = slice(None) if full else columns(shapes[g], 1)
+            diag_y(g, zz, full).wait_recv()
+            add(own[g].at[zz, y, 1 - x, :, part], from_dy[g].at[zz, :, part])
+            x_copy(g, zz).start()
+
+        if not with_tiles:
+            take_x()
+            take_y(False)
+            return
+
+        @pl.when(x == 0)
+        def _():
+            take_y(False)
+
+        @pl.when(x == 1)
+        def _():
+            take_x()
+            take_y(True)
+
+    def stage_line(g, t):
         zz = visit(t, z, planes)
         x_copy(g, zz).wait_recv()
         y_copy(g, zz).wait_recv()
         here = own[g].at[zz, y, x]
-        if t > 0:
+
+        @pl.when(t > 0)
+        def _():
             add(here, from_x[g].at[zz], from_y[g].at[zz])
             farther = jnp.where(zz > z, z > 0, z < planes - 1)
 
@@ -808,7 +842,8 @@
             def _():
                 z_copy(g, zz, False).start()
 
-        else:
+        @pl.when(t == 0)
+        def _():
             outs[g][...] = (
                 here[...].astype(f32)
                 + from_x[g][zz].astype(f32)
@@ -825,54 +860,76 @@
                 z_arrival(g, planes).wait_recv()
                 outs[g][...] += from_z[g][planes].astype(f32)
 
-    lag_plane, lag_line = lags
-    for i in range(len(items) + lag_line):
-        if i < len(items):
-            stage_core(*items[i])
-        if 0 <= i - lag_plane < len(items):
-            stage_plane(*items[i - lag_plane])
-        if 0 <= i - lag_line < len(items):
-            stage_line(*items[i - lag_line])
-    for t, g in items:
+    @pl.loop(0, planes + 2)
+    def _(r):
+        t = planes - 1 - r
+        for g in range(n):
+
+            @pl.when(r < planes)
+            def _():
+                stage_core(g, t)
+
+            @pl.when((r >= 1) & (r < planes + 1))
+            def _():
+                stage_plane(g, t + 1)
+
+            @pl.when(r >= 2)
+            def _():
+                stage_line(g, t + 2)
+
+            if with_tiles and g % 2 == 0:
+                work(r * 2 + g // 2)
+
+    @pl.loop(0, planes)
+    def _(r):
+        t = planes - 1 - r
         zz = visit(t, z, planes)
-        core_copy(g, zz).wait_send()
-        diag(g, zz, 0).wait_send()
-        diag(g, zz, 1).wait_send()
-        x_copy(g, zz).wait_send()
-        y_copy(g, zz).wait_send()
-        if t > 0:
-            z_copy(g, zz, True).wait_send()
+        for g in range(n):
+            core_copy(g, zz).wait_send()
+
+            def even():
+                diag_x(g, zz).wait_send()
+                diag_y(g, zz, False).wait_send()
+
+            lean_or_even(lambda: diag_y(g, zz, True).wait_send(), even)
+            x_copy(g, zz).wait_send()
+            y_copy(g, zz).wait_send()
+
+            @pl.when(t > 0)
+            def _():
+                z_copy(g, zz, True).wait_send()
+
     if with_tiles:
-        load_mine.wait()
-        send_b.wait()
-
-        @pl.when(x == 0)
-        def _():
-            send_back.wait_recv()
+        for s in range(seqs):
+            send_b(s).wait()
+
+            @pl.when(x == 0)
+            def _():
+                send_back(s).wait_recv()
+
+            @pl.when(x == 1)
+            def _():
+                send_d(s).wait_send()
+                send_back(s).wait_send()
 
         @pl.when(x == 1)
         def _():
-            send_d.wait_send()
-            send_back.wait_send()
-
-        @pl.when(x == 1)
-        def _():
-            back[...] = jnp.zeros_like(back)
-
-        @pl.loop(0, mine.shape[1] * rows // 32)
+            chip[...] = jnp.zeros_like(chip)
+
+        @pl.loop(0, seqs * rows // 32)
         def _(i):
             seq = lax.div(i, rows // 32)
             at = pl.ds(pl.multiple_of(lax.rem(i, rows // 32) * 32, 32), 32)
             flat = pl.ds(pl.multiple_of(i * 32, 32), 32)
             cos_rows, sin_rows = cos_table[flat, :], sin_table[flat, :]
-            for k in range(mine.shape[3] // 128):
+            for k in range(pairs):
                 lanes = pl.ds(k * 128, 128)
 
                 def summed(kind):
                     return (
                         mine[kind, seq, at, lanes].astype(f32)
                         + from_b[kind, seq, at, lanes].astype(f32)
-                        + back[kind, seq, at, lanes].astype(f32)
+                        + chip[kind, seq, at, lanes].astype(f32)
                     )
 
                 d_key[flat, lanes] = turned(summed(0), cos_rows, sin_rows, -1.0).astype(jnp.bfloat16)
@@ -881,7 +938,7 @@
                 first_grad[flat, lanes] = half
 
 
-def scatter_sum(planes, partials, lags, collective_id, tiles=None, angles=None):
+def scatter_sum(planes, partials, collective_id, attention=None):
     n = len(partials)
     partials = [
         p.reshape(planes, 2, 2, 2, p.shape[0] // (planes * 8), p.shape[1]) for p in partials
@@ -890,36 +947,42 @@
     types = [p.dtype for p in partials]
     dma = pltpu.SemaphoreType.DMA
 
-    def boxes(lead, half=None):
+    def boxes(lead, narrow=False):
         out = []
         for s, d in zip(shapes, types):
-            cut = s[1] // 2 // 128 * 128
-            width = s[1] if half is None else (cut if half == 0 else s[1] - cut)
+            width = s[1] // 2 // 128 * 128 if narrow else s[1]
             out.append(pltpu.VMEM((*lead, s[0], width), d))
         return out
 
     extra, extra_out, extra_scratch = [], [], []
-    if tiles is not None:
-        extra = [*tiles, *angles]
-        box = tiles[0].shape
-        flat = (box[1] * box[2], box[3])
+    if attention is not None:
+        extra = list(attention)
+        box = attention[2].shape
+        seqs, rows, width = box[1:]
+        flat = (seqs * rows, width)
         extra_out = [
+            jax.ShapeDtypeStruct(box[1:], jnp.bfloat16),
             jax.ShapeDtypeStruct(flat, jnp.bfloat16),
             jax.ShapeDtypeStruct(flat, jnp.bfloat16),
             jax.ShapeDtypeStruct(flat, jnp.float32),
         ]
-        extra_scratch = [pltpu.VMEM(box, jnp.bfloat16)] * 5 + [dma((2,)), dma((3,)), dma((3,))]
+        extra_scratch = [
+            *[pltpu.VMEM(box, jnp.bfloat16)] * 6,
+            dma((3, seqs)),
+            dma((3, seqs)),
+            *attend_back_scratch(rows),
+        ]
     return pl.pallas_call(
-        functools.partial(scatter_kernel, planes, shapes, lags, bool(extra)),
+        functools.partial(scatter_kernel, planes, shapes, bool(extra)),
         out_shape=[jax.ShapeDtypeStruct(s, jnp.float32) for s in shapes] + extra_out,
-        in_specs=[pl.BlockSpec(memory_space=pl.ANY)] * (n + len(extra[:4]))
-        + [pl.BlockSpec(memory_space=pltpu.VMEM)] * len(extra[4:]),
+        in_specs=[pl.BlockSpec(memory_space=pl.ANY)] * n
+        + [pl.BlockSpec(memory_space=pltpu.VMEM)] * len(extra),
         out_specs=[pl.BlockSpec(memory_space=pltpu.VMEM)] * (n + len(extra_out)),
         scratch_shapes=[
             *boxes((planes, 2, 2)),
             *boxes((planes, 2, 2)),
-            *boxes((planes,), 0),
-            *boxes((planes,), 1),
+            *boxes((planes,), True),
+            *boxes((planes,)),
             *boxes((planes,)),
             *boxes((planes,)),
             *boxes((planes + 1,)),
@@ -937,7 +1000,7 @@
             *extra_scratch,
         ],
         compiler_params=pltpu.CompilerParams(
-            collective_id=collective_id, has_side_effects=True, vmem_limit_bytes=62 * 2**20
+            collective_id=collective_id, has_side_effects=True, vmem_limit_bytes=67043328
         ),
         name="gradient_scatter",
     )(*partials, *extra)
@@ -1023,13 +1086,13 @@
     d_residual_low = d_residual.astype(bf16)
     d_out = by_rows(context, d_residual_low)
     d_context = back(d_residual_low, w_out).astype(bf16).reshape(local)
-    d_query, *d_tiles = attend_back(
-        starts, query_rot, tiles, context3, d_context, log_total, cos_table, sin_table
+    s_down, s_gate, s_up, s_out, d_query, d_key, d_value, first_grad = scatter_sum(
+        planes,
+        [d_down, d_gate_weight, d_up_weight, d_out],
+        2,
+        [starts, query_rot, *tiles, context3, d_context, log_total, cos_table, sin_table],
     )
     d_query = d_query.reshape(flat)
-    s_down, s_gate, s_up, s_out, d_key, d_value, first_grad = scatter_sum(
-        planes, [d_down, d_gate_weight, d_up_weight, d_out], (4, 8), 2, d_tiles, (cos_table, sin_table)
-    )
     d_wq = by_rows(normed_one, d_query)
     d_wk = by_rows(normed_one, d_key)
     d_wv = by_rows(normed_one, d_value)
@@ -1046,7 +1109,7 @@
     d_gains = jnp.stack([d_attn_gain, d_ffn_gain]).reshape(2, devices, share)
     d_gains = jnp.zeros((devices, 8, 256), f32).at[:, :2, :share].set(d_gains.transpose(1, 0, 2))
     s_wq, s_wk, s_wv, s_gains = scatter_sum(
-        planes, [d_wq, d_wk, d_wv, d_gains.reshape(devices * 8, 256)], (4, 8), 3
+        planes, [d_wq, d_wk, d_wv, d_gains.reshape(devices * 8, 256)], 3
     )
     return (
         output.reshape(local),

time: 534 us -> 478 us (0.90)
  Pallas kernels: 412 us -> 374 us
  matrix products: 89.4 us -> 72.1 us
    pallas_call x3 -> x2, Pallas kernels: 221 us -> 183 us  [scatter_sum(): pl.pallas_call(functools.partial(scatter_kernel, planes, shapes, bool(ext...]
    dot_general x7, matrix products: 35.3 us -> 26 us  [on_device(): back = lambda a, b: lax.dot_general(a, b, NT, preferred_element_type=f32)]
where the time goes in v3:
time: 478 us; the launch traced here: 474 us
  Pallas kernels  374 us (78%)
  matrix products  72.1 us (15%)
  local copies, waits for them, and re-layouts  17.3 us (4%)
  other arithmetic  9.5 us (2%)
    pallas_call x2, Pallas kernels, scatter_sum(): pl.pallas_call(functools.partial(scatter_kernel, planes, shapes, bool(ext...  183 us
    pallas_call x2, Pallas kernels, gather(): pl.pallas_call(functools.partial(gather_kernel, planes, shapes, pair is n...  164 us
    dot_general x7, matrix products, on_device(): lax.dot_general(a, b, TN, preferred_element_type=f32).astype(bf16)  27.2 us
    dot_general x7, matrix products, on_device(): back = lambda a, b: lax.dot_general(a, b, NT, preferred_element_type=f32)  26 us
    pallas_call x1, Pallas kernels, attend(): pl.pallas_call(attend_kernel, grid=(seqs, pairs), in_specs=[pl.BlockSpec(...  17.7 us
    unnamed x91, local copies, waits for them, and re-layouts  10.1 us

profile of v3, /device:TPU:0, one launch (start us, length us, event | category | flops | bytes accessed | tf_op | source)
XLA Modules:
  0.0 473.9 jit_solution(813232486223200980)
XLA Ops:
  8.7 37.0 %weight_gather.2 = (bf16[1,4,2,2,2,16,128]{6,5,4,3,2,1,0:T(8,128)(2,1)}, bf16[1,4,2,2,2,32,1024]{6,5,4,3,2,1,0:T(8,128)(2,1)}, bf16[1,4,2,2,2,32,1024]{6,5,4,3,2...) custom-call(bf16[1,16,128]{2,1,0:T(8,128)(2,1)} %copy-done.21, bf16[1,32,1024]{2,1,0:T(8,128)(2,1)} %bitcast.146, ...), custom_call_target="tpu_custom_call" | custom-call | tf_op jit(solution)/shard_map/weight_gather/pallas_call | solution.py:537
  48.9 8.7 %project.1 = (bf16[512,1024]{1,0:T(8,128)(2,1)}, bf16[512,1024]{1,0:T(8,128)(2,1)}, bf16[2,512,1024]{2,1,0:T(8,128)(2,1)}) custom-call(bf16[512,1024]{1,0:T(8,128)(2,1)} %bitcast.117, bf16[512,1024]{1,0:T(8,128)(2,1)} %bitcast.142, bf16[1,1024]{1,0:T(2,128)(2,1)} %reshape_squeeze.4.gain, bf16[1024,1024]{1,0:T(8,128)(2,1)} %bitcast.132, ...), custom_call_target="tpu_custom_call" | custom-call | tf_op jit(solution)/shard_map/project/pallas_call | solution.py:84
  57.6 127.0 %weight_gather.3 = (bf16[1,4,2,2,2,32,1024]{6,5,4,3,2,1,0:T(8,128)(2,1)}, bf16[1,4,2,2,2,32,2816]{6,5,4,3,2,1,0:T(8,128)(2,1)}, bf16[1,4,2,2,2,32,2816]{6,5,4,3,...) custom-call(bf16[1,32,1024]{2,1,0:T(8,128)(2,1)} %bitcast.149, ...), custom_call_target="tpu_custom_call" | custom-call | tf_op jit(solution)/shard_map/weight_gather/pallas_call | solution.py:537
  184.6 17.7 %attend.1 = (bf16[2,256,1024]{2,1,0:T(8,128)(2,1)}, f32[2,8,1,512]{3,2,1,0:T(1,128)}) custom-call(s32[2,1,256]{2,1,0:T(1,128)} %reshape.310.starts.refs_4_, bf16[2,256,1024]{2,1,0:T(8,128)(2,1)} %bitcast.124, bf16[2,2,256,1024]{3,2,1,0:T(8,128)(2,1)} %bitcast.115, bf16[2,2,256,1024]{3,2,1,0:T(8,128)(2,1)} %get-tuple-element.93.tile_b.refs_7_, ...), custom_call_target="tpu_custom_call" | custom-call | tf_op jit(solution)/shard_map/attend/pallas_call | solution.py:215
  202.3 2.8 multiply_reduce_fusion.3
  205.4 5.0 %fusion.20 = f32[512,2816]{1,0:T(8,128)} fusion(bf16[512,1024]{1,0:T(8,128)(2,1)S(1)} %multiply_convert_fusion.1, bf16[1024,2816]{1,0:T(8,128)(2,1)S(1)} %bitcast.163), kind=kOutput, calls=%fused_computation.70 | convolution fusion | flops 2952790016 | bytes 12582912 | tf_op jit(solution)/shard_map/dot_general | solution.py:1064
  210.4 5.0 %fusion.19 = f32[512,2816]{1,0:T(8,128)} fusion(bf16[512,1024]{1,0:T(8,128)(2,1)S(1)} %multiply_convert_fusion.1, bf16[1024,2816]{1,0:T(8,128)(2,1)S(1)} %bitcast.167), kind=kOutput, calls=%fused_computation.69 | convolution fusion | flops 2952790016 | bytes 12582912 | tf_op jit(solution)/shard_map/dot_general | solution.py:1063
  215.4 10.4 %fusion.3 = (bf16[512,2816]{1,0:T(8,128)(2,1)}, bf16[512,2816]{1,0:T(8,128)(2,1)}, bf16[512,2816]{1,0:T(8,128)(2,1)}) fusion(f32[512,2816]{1,0:T(8,128)} %fusion.19, f32[512,2816]{1,0:T(8,128)} %fusion.20, bf16[2816,1024]{1,0:T(8,128)(2,1)S(1)} %bitcast.171, bf16[512,1024]{1,0:T(8,128)(2,1)S(1)} %bitcast.136), kind=kOutput, calls=%fused_computation.5 | convolution fusion | flops 2974416896 | bytes 27000832 | tf_op jit(solution)/shard_map/dot_general | solution.py:1042
  225.8 6.1 %add_convert_fusion = bf16[512,1024]{1,0:T(8,128)(2,1)} fusion(f32[512,1024]{1,0:T(8,128)S(1)} %get-tuple-element.130, bf16[512,2816]{1,0:T(8,128)(2,1)} %get-tuple-element.122, bf16[2816,1024]{1,0:T(8,128)(2,1)S(1)} %bitcast.172), kind=kOutput, calls=%fused_computation.26 | convolution fusion | flops 2953838592 | bytes 11796480 | tf_op jit(solution)/shard_map/dot_general | solution.py:1066
  232.0 3.2 fusion.21
  235.2 3.5 multiply_reduce_fusion
  240.3 2.4 convolution_convert_fusion.7
  243.4 4.0 convolution_convert_fusion.6
  247.4 5.1 %convolution_convert_fusion = bf16[1024,2816]{1,0:T(8,128)(2,1)} fusion(bf16[512,1024]{1,0:T(8,128)(2,1)S(1)} %copy-done.8, bf16[512,2816]{1,0:T(8,128)(2,1)S(1)} %copy-done.29), kind=kOutput, calls=%fused_computation.9 | convolution fusion | flops 2955673600 | bytes 9699328 | tf_op jit(solution)/shard_map/dot_general | solution.py:1041
  252.5 5.0 %convolution_convert_fusion.1 = bf16[1024,2816]{1,0:T(8,128)(2,1)} fusion(bf16[512,1024]{1,0:T(8,128)(2,1)S(1)} %copy-done.8, bf16[512,2816]{1,0:T(8,128)(2,1)S(1)} %copy-done.32), kind=kOutput, calls=%fused_computation.10 | convolution fusion | flops 2955673600 | bytes 9699328 | tf_op jit(solution)/shard_map/dot_general | solution.py:1041
  257.5 5.2 %convolution_convert_fusion.2 = bf16[2816,1024]{1,0:T(8,128)(2,1)} fusion(bf16[512,2816]{1,0:T(8,128)(2,1)S(1)} %copy-done.30, bf16[512,1024]{1,0:T(8,128)(2,1)S(1)} %bitcast.137), kind=kOutput, calls=%fused_computation.11 | convolution fusion | flops 2955673600 | bytes 9699328 | tf_op jit(solution)/shard_map/dot_general | solution.py:1041
  262.7 149.5 %gradient_scatter.2 = (f32[88,1024]{1,0:T(8,128)}, f32[32,2816]{1,0:T(8,128)}, f32[32,2816]{1,0:T(8,128)}, f32[32,1024]{1,0:T(8,128)}, bf16[2,256,1024]{2,1,0:T(...) custom-call(bf16[4,2,2,2,88,1024]{5,4,3,2,1,0:T(8,128)(2,1)} %bitcast.123, ...), custom_call_target="tpu_custom_call" | custom-call | tf_op jit(solution)/shard_map/gradient_scatter/pallas_call | solution.py:975
  412.3 3.3 fusion.23
  419.8 1.9 fusion.6
  422.6 2.7 convolution_convert_fusion.3
  425.3 2.6 convolution_convert_fusion.5
  427.9 2.6 convolution_convert_fusion.4
  430.5 33.7 %gradient_scatter.3 = (f32[32,1024]{1,0:T(8,128)}, f32[32,1024]{1,0:T(8,128)}, f32[32,1024]{1,0:T(8,128)}, f32[8,256]{1,0:T(8,128)}) custom-call(bf16[4,2,2,2,32,1024]{5,4,3,2,1,0:T(8,128)(2,1)} %bitcast.129, bf16[4,2,2,2,32,1024]{5,4,3,2,1,0:T(8,128)(2,1)} %bitcast.130, bf16[4,2,2,2,32,1024]{5,4,3,2,1,0:T(8,128)(2,1)} %bitcast.128, ...), custom_call_target="tpu_custom_call" | custom-call | tf_op jit(solution)/shard_map/gradient_scatter/pallas_call | solution.py:975
  465.5 3.3 copy.48
  (126 shorter events, 24.8 us)
Async XLA Ops:
  184.5 17.7 %copy-start = (bf16[2,256,1024]{2,1,0:T(8,128)(2,1)S(1)}, bf16[2,256,1024]{2,1,0:T(8,128)(2,1)}, u32[]{:S(2)}) copy-start(bf16[2,256,1024]{2,1,0:T(8,128)(2,1)} %param.19) | copy-start | bytes 3145732
  184.6 17.7 %copy-start.23 = (bf16[1,4,2,2,2,32,1024]{6,5,4,3,2,1,0:T(8,128)(2,1)S(1)}, bf16[1,4,2,2,2,32,1024]{6,5,4,3,2,1,0:T(8,128)(2,1)}, u32[]{:S(2)}) copy-start(bf16[1,4,2,2,2,32,1024]{6,5,4,3,2,1,0:T(8,128)(2,1)} %get-tuple-element.97) | copy-start | bytes 6291460
  205.1 5.3 %slice-start.2 = ((s8[5767168]{0:T(1024)(128)(4,1)}), s8[4194304]{0:T(1024)(128)(4,1)S(1)}, s32[]{:S(2)}) async-start(s8[5767168]{0:T(1024)(128)(4,1)} %bitcast.165), calls=%async_computation.2 | async-start | bytes 8388608
  205.4 5.0 %copy-start.7 = (bf16[512,1024]{1,0:T(8,128)(2,1)}, bf16[512,1024]{1,0:T(8,128)(2,1)S(1)}, u32[]{:S(2)}) copy-start(bf16[512,1024]{1,0:T(8,128)(2,1)S(1)} %multiply_convert_fusion.1) | copy-start | bytes 3145732
  205.4 5.0 %slice-start.3 = ((s8[5767168]{0:T(1024)(128)(4,1)}), s8[1572864]{0:T(1024)(128)(4,1)S(1)}, s32[]{:S(2)}) async-start(s8[5767168]{0:T(1024)(128)(4,1)} %bitcast.165), calls=%async_computation.3 | async-start | bytes 3145728
  205.4 10.0 %slice-start.4 = ((s8[5767168]{0:T(1024)(128)(4,1)}), s8[4194304]{0:T(1024)(128)(4,1)S(1)}, s32[]{:S(2)}) async-start(s8[5767168]{0:T(1024)(128)(4,1)} %bitcast.169), calls=%async_computation.4 | async-start | bytes 8388608
  210.4 5.0 %copy-start.6 = (bf16[2,256,1024]{2,1,0:T(8,128)(2,1)S(1)}, bf16[2,256,1024]{2,1,0:T(8,128)(2,1)}, u32[]{:S(2)}) copy-start(bf16[2,256,1024]{2,1,0:T(8,128)(2,1)} %param.21) | copy-start | bytes 3145732
  210.4 5.0 %slice-start.5 = ((s8[5767168]{0:T(1024)(128)(4,1)}), s8[1572864]{0:T(1024)(128)(4,1)S(1)}, s32[]{:S(2)}) async-start(s8[5767168]{0:T(1024)(128)(4,1)} %bitcast.169), calls=%async_computation.5 | async-start | bytes 3145728
  225.8 6.1 %copy-start.31 = (bf16[512,2816]{1,0:T(8,128)(2,1)S(1)}, bf16[512,2816]{1,0:T(8,128)(2,1)}, u32[]{:S(2)}) copy-start(bf16[512,2816]{1,0:T(8,128)(2,1)} %get-tuple-element.121) | copy-start | bytes 8650756
  232.0 3.2 copy-start.28
  240.3 3.1 copy-start.2
  243.4 4.0 copy-start.8
  243.4 4.0 copy-start.29
  247.4 5.1 %copy-start.32 = (bf16[512,2816]{1,0:T(8,128)(2,1)S(1)}, bf16[512,2816]{1,0:T(8,128)(2,1)}, u32[]{:S(2)}) copy-start(bf16[512,2816]{1,0:T(8,128)(2,1)} %get-tuple-element.121) | copy-start | bytes 8650756
  252.5 5.0 %copy-start.30 = (bf16[512,2816]{1,0:T(8,128)(2,1)S(1)}, bf16[512,2816]{1,0:T(8,128)(2,1)}, u32[]{:S(2)}) copy-start(bf16[512,2816]{1,0:T(8,128)(2,1)} %get-tuple-element.122) | copy-start | bytes 8650756
  412.3 3.4 copy-start.5
  412.3 3.4 copy-start.27
  465.5 3.3 copy-start.16
  465.5 4.0 copy-start.15
  465.5 4.6 copy-start.14
  465.5 5.3 %copy-start.13 = (f32[32,1024]{1,0:T(8,128)S(1)}, f32[32,1024]{1,0:T(8,128)}, u32[]{:S(2)}) copy-start(f32[32,1024]{1,0:T(8,128)} %get-tuple-element.154) | copy-start | bytes 393220
  465.5 5.9 %copy-start.12 = (f32[32,2816]{1,0:T(8,128)S(1)}, f32[32,2816]{1,0:T(8,128)}, u32[]{:S(2)}) copy-start(f32[32,2816]{1,0:T(8,128)} %get-tuple-element.156) | copy-start | bytes 1081348
  465.5 6.6 %copy-start.11 = (f32[32,2816]{1,0:T(8,128)S(1)}, f32[32,2816]{1,0:T(8,128)}, u32[]{:S(2)}) copy-start(f32[32,2816]{1,0:T(8,128)} %get-tuple-element.157) | copy-start | bytes 1081348
  468.8 4.1 copy-start.10
  (15 other events, 31.2 us)
